TPU v7x, 32 devices: a whole 2x2x4 slice. The times are simulated.
32 devices in a mesh: gx: 2 (over y), gy: 4 (over z), gz: 4 (over x, core).
Axes of the slice: x: 2, y: 2, z: 4, core: 2. Of those that a mesh axis runs over, the one named last changes fastest.
Arguments:
- density: float32 [64, 64, 512], P('gx', 'gy', 'gz'), may hold values from -8 to 8
Outputs:
- potential: float32 [64, 64, 512], P('gx', 'gy', 'gz')
All inputs are finite; a program needn't handle non-finite values.
Results may differ from a plain program's by a relative error of at most 0.00002.
Values sent between devices are 32-bit elements; how exact they have to be, the bound alone decides.
A program may use at most 128 MiB of HBM per device.

v0:
```python
import functools

import jax
import jax.numpy as jnp
from jax import lax
from jax.experimental import pallas as pl
from jax.experimental.pallas import tpu as pltpu
from jax.sharding import PartitionSpec as P

LEVELS = 7
CSWEEPS = 4
rsd_beta = 0.5
centre = 4.0 + 2.0 * (1.0 + rsd_beta)
along = 1.0 + rsd_beta
inverse = 1.0 / centre
F32 = jnp.float32
LANES = 128
AXES = ("gx", "gy", "gz")
STEPS_XY = [(dx, dy) for dx in (-1, 0, 1) for dy in (-1, 0, 1) if (dx, dy) != (0, 0)]


def up_to(value, unit):
    return -(-value // unit) * unit


class Split:
    def __init__(self, block, margins, counts):
        self.block, self.margins, self.counts = block, margins, counts
        self.planes = block[0] + 2 * margins[0]
        self.rows = up_to(block[1] + 2 * margins[1], 8)
        self.lanes = up_to(block[2] + 2 * margins[2], LANES)
        self.per = LANES // margins[2]
        self.packs = -(-self.planes // self.per)
        self.shape = (self.planes, self.rows, self.lanes)

    def scratch(self):
        land_x = (2, self.margins[0], self.block[1], LANES)
        land_y = (2, self.planes, self.margins[1], LANES)
        stage_y = (2, self.block[0], self.margins[1], LANES)
        packed = (2, self.packs, self.rows, LANES)
        one = [
            pltpu.VMEM(land_x, F32),
            pltpu.VMEM(land_x, F32),
            pltpu.VMEM(land_y, F32),
            pltpu.VMEM(stage_y, F32),
            pltpu.VMEM(packed, F32),
            pltpu.VMEM(packed, F32),
            pltpu.SemaphoreType.DMA((10,)),
            pltpu.SemaphoreType.DMA((10,)),
        ]
        own = [
            pltpu.VMEM(self.shape, F32),
            pltpu.VMEM((self.planes + 2,) + self.shape[1:], F32),
            pltpu.VMEM((2,) + self.shape[1:], jnp.int32),
        ]
        return own, one, list(one)


class Whole:
    def __init__(self, size):
        self.size = size
        self.rows = up_to(size[1], 8)
        self.lanes = up_to(size[2], LANES)
        self.shape = (size[0], self.rows, self.lanes)

    def scratch(self):
        return [
            pltpu.VMEM(self.shape, F32),
            pltpu.VMEM((self.shape[0] + 2,) + self.shape[1:], F32),
        ]


def iota(shape, dim):
    return lax.broadcasted_iota(jnp.int32, shape, dim)


def pieces(value):
    high = value.astype(jnp.bfloat16)
    rest = value - high.astype(F32)
    middle = rest.astype(jnp.bfloat16)
    return high, middle, (rest - middle.astype(F32)).astype(jnp.bfloat16)


def dot(value, chosen):
    chosen = chosen.astype(jnp.bfloat16)
    parts = [jnp.dot(part, chosen, preferred_element_type=F32) for part in pieces(value)]
    return parts[0] + (parts[1] + parts[2])


def dot_rows(chosen, value):
    return jnp.dot(chosen, value, precision=lax.Precision.HIGHEST, preferred_element_type=F32)


def local_of(index, length, margin, total):
    return jnp.where(index < total - margin, index, index - total)


def beside_sum(below, here, above, size, rows, lanes):
    down, up = pltpu.roll(here, 1, 0), pltpu.roll(here, rows - 1, 0)
    left, right = pltpu.roll(here, 1, 1), pltpu.roll(here, lanes - 1, 1)
    if size is not None:
        if size[1] == rows:
            row = iota(here.shape, 0)
            down = jnp.where(row == 0, 0.0, down)
            up = jnp.where(row == rows - 1, 0.0, up)
        if size[2] == lanes:
            lane = iota(here.shape, 1)
            left = jnp.where(lane == 0, 0.0, left)
            right = jnp.where(lane == lanes - 1, 0.0, right)
    return (below + above + (down + up)) + along * (left + right)


def chunk_of(planes, most):
    if planes <= most:
        return planes
    return max([number for number in range(2, most + 1, 2) if planes % number == 0])


def for_planes(first, planes, most, body):
    chunk = chunk_of(planes, most)
    if chunk == planes:
        body(first, planes)
        return

    def step(number, carry):
        body(first + number * chunk, chunk)
        return carry

    lax.fori_loop(0, planes // chunk, step, 0)


def half(field, source, masks, colour, keep, size, shape, most, skip=0):
    planes, rows, lanes = shape

    def body(start, count):
        before, here = field[start], field[start + 1]
        for number in range(count):
            after = field[start + number + 2]
            total = beside_sum(before, here, after, size, rows, lanes)
            update = (source[start + number] + total) * inverse
            chosen = masks((number + skip + colour) % 2, keep(start + number))
            field[start + number + 1] = jnp.where(chosen, update, here)
            before, here = here, after

    for_planes(skip, planes - 2 * skip, most, body)


def first_half(field, source, masks, keep, shape, most):
    planes, rows, lanes = shape
    field[0] = jnp.zeros((rows, lanes), F32)
    field[planes + 1] = jnp.zeros((rows, lanes), F32)

    def body(start, count):
        for number in range(count):
            chosen = masks(number % 2, keep(start + number))
            field[start + number + 1] = jnp.where(chosen, source[start + number] * inverse, 0.0)

    for_planes(0, planes, most, body)


def sweeps(field, source, masks, keep, size, shape, most, halves, skips=None):
    for number, colour in enumerate(halves):
        skip = 0 if skips is None else skips[number]
        half(field, source, masks, colour, keep, size, shape, most, skip)


def restricted(field, source, pairs, first, block, size, shape, most):
    planes, rows, lanes = shape
    height = pairs.shape[1]
    count_x, count_y, count_z = block
    top = min(height, up_to(count_y, 8))
    if height > top:
        pairs[0 : count_x // 2, top:height] = jnp.zeros((count_x // 2, height - top, LANES), F32)

    def body(start, count):
        old = [field[first + start + number] for number in range(count + 2)]
        parts = []
        for number in range(count):
            here = old[number + 1]
            total = beside_sum(old[number], here, old[number + 2], size, rows, lanes)
            rest = source[first + start + number] - centre * here + total
            parts.append(rest[:top, :LANES])
        half_start = start // 2 if isinstance(start, int) else lax.div(start, 2)
        for number in range(count // 2):
            both = parts[2 * number] + parts[2 * number + 1]
            if top > count_y:
                both = jnp.where(iota(both.shape, 0) < count_y, both, 0.0)
            pairs[half_start + number, 0:top] = both

    for_planes(0, count_x, most, body)
    number = count_x // 2
    even = pairs[0:number, pl.ds(0, height // 2, stride=2), :]
    odd = pairs[0:number, pl.ds(1, height // 2, stride=2), :]
    lane, column = iota((LANES, LANES), 0), iota((LANES, LANES), 1)
    down = jnp.where((lane // 2 == column) & (lane < count_z), 0.5, 0.0).astype(F32)
    flat = (even + odd).reshape(number * (height // 2), LANES)
    return dot(flat, down).reshape(number, height // 2, LANES)


def device(place, steps):
    return tuple(place[which] + steps[which] for which in range(3))


def exists(place, steps, counts):
    found = None
    for which in range(3):
        if steps[which] == 0:
            continue
        other = place[which] + steps[which]
        here = (other >= 0) & (other < counts[which])
        found = here if found is None else found & here
    return found


class Exchange:
    def __init__(self, level, place, array, offset, refs):
        self.level, self.place, self.array, self.offset = level, place, array, offset
        (self.stage_x, self.land_x, self.land_y, self.stage_y) = refs[:4]
        (self.stage_z, self.land_z, self.sent, self.got) = refs[4:]

    def xy(self, number):
        level = self.level
        dx, dy = STEPS_XY[number]
        margin, length = level.margins[0], level.block[0]
        place = {1: 0, 0: margin, -1: margin + length}[dx]
        count = length if dx == 0 else margin
        origin = length - margin if dx == 1 else 0
        if dy == 0:
            source = self.stage_x.at[(dx + 1) // 2]
            target = self.land_x.at[(dx + 1) // 2]
        else:
            source = self.stage_y.at[(dy + 1) // 2, pl.ds(origin, count)]
            target = self.land_y.at[(dy + 1) // 2, pl.ds(place, count)]
        return (dx, dy, 0), (place, count), pltpu.make_async_remote_copy(
            src_ref=source,
            dst_ref=target,
            send_sem=self.sent.at[number],
            recv_sem=self.got.at[number],
            device_id=device(self.place, (dx, dy, 0)),
            device_id_type=pl.DeviceIdType.MESH,
        )

    def start_xy(self):
        level, array = self.level, self.array
        low = self.offset + level.margins[0]
        length, rows, margin = level.block[0], level.block[1], level.margins
        self.stage_y[0] = array[low : low + length, 0 : margin[1], 0:LANES]
        self.stage_y[1] = array[low : low + length, rows - margin[1] : rows, 0:LANES]
        self.stage_x[0] = array[low : low + margin[0], 0:rows, 0:LANES]
        self.stage_x[1] = array[low + length - margin[0] : low + length, 0:rows, 0:LANES]
        for number in range(8):
            steps, _, copy = self.xy(number)

            @pl.when(exists(self.place, steps, level.counts))
            def _():
                copy.start()

    def finish_xy(self):
        level, array = self.level, self.array
        rows, margin = level.block[1], level.margins[1]
        for number in range(8):
            steps, (place, count), copy = self.xy(number)
            back = tuple(-step for step in steps)

            @pl.when(exists(self.place, back, level.counts))
            def _():
                copy.wait_recv()
                low = self.offset + place
                if steps[1] == 0:
                    array[low : low + count, 0:rows, 0:LANES] = self.land_x[(steps[0] + 1) // 2]
                else:
                    first = level.rows - margin if steps[1] == 1 else rows
                    side = (steps[1] + 1) // 2
                    array[low : low + count, first : first + margin, 0:LANES] = self.land_y[
                        side, place : place + count
                    ]

    def z(self, side):
        return pltpu.make_async_remote_copy(
            src_ref=self.stage_z.at[side],
            dst_ref=self.land_z.at[side],
            send_sem=self.sent.at[8 + side],
            recv_sem=self.got.at[8 + side],
            device_id=device(self.place, (0, 0, 2 * side - 1)),
            device_id_type=pl.DeviceIdType.MESH,
        )

    def start_z(self):
        level, array = self.level, self.array
        margin, length = level.margins[2], level.block[2]
        lane = iota((level.rows, LANES), 1)
        for side in range(2):
            first = length - margin if side == 1 else 0
            for pack in range(level.packs):
                total = jnp.zeros((level.rows, LANES), F32)
                for number in range(min(level.per, level.planes - pack * level.per)):
                    plane = array[self.offset + pack * level.per + number, :, 0:LANES]
                    moved = pltpu.roll(plane, (number * margin - first) % LANES, 1)
                    total = jnp.where(lane // margin == number, moved, total)
                self.stage_z[side, pack] = total
        for side in range(2):
            @pl.when(exists(self.place, (0, 0, 2 * side - 1), level.counts))
            def _():
                self.z(side).start()

    def finish_z(self):
        level, array = self.level, self.array
        margin, length = level.margins[2], level.block[2]
        base = level.lanes - LANES
        lane = iota((level.rows, LANES), 1)
        have = []
        for side in range(2):
            there = exists(self.place, (0, 0, 1 - 2 * side), level.counts)
            have.append(there)

            @pl.when(there)
            def _():
                self.z(side).wait_recv()

        above = length - base
        take_above = (lane >= above) & (lane < above + margin) & have[0]
        take_below = (lane >= LANES - margin) & have[1]
        for pack in range(level.packs):
            from_above, from_below = self.land_z[0, pack], self.land_z[1, pack]
            for number in range(min(level.per, level.planes - pack * level.per)):
                plane = self.offset + pack * level.per + number
                high = pltpu.roll(from_above, (above - number * margin) % LANES, 1)
                low = pltpu.roll(from_below, (LANES - margin - number * margin) % LANES, 1)
                value = array[plane, :, base : level.lanes]
                value = jnp.where(take_above, high, value)
                array[plane, :, base : level.lanes] = jnp.where(take_below, low, value)

    def drain(self):
        for number in range(8):
            steps, _, copy = self.xy(number)

            @pl.when(exists(self.place, steps, self.level.counts))
            def _():
                copy.wait_send()

        for side in range(2):
            @pl.when(exists(self.place, (0, 0, 2 * side - 1), self.level.counts))
            def _():
                self.z(side).wait_send()


def solve_whole(levels, refs, pairs, number):
    level = levels[number]
    source, field = refs[number]
    planes, rows, lanes = level.shape
    row, lane = iota((rows, lanes), 0), iota((rows, lanes), 1)
    inside = (row < level.size[1]) & (lane < level.size[2])
    choices = [inside & ((row + lane) % 2 == colour) for colour in range(2)]

    def masks(which, keep):
        return choices[which]

    def keep(plane):
        return None

    first_half(field, source, masks, keep, level.shape, 16)
    if number == len(levels) - 1:
        sweeps(field, source, masks, keep, level.size, level.shape, 16, (1,) + (0, 1) * (CSWEEPS - 1))
        return
    sweeps(field, source, masks, keep, level.size, level.shape, 16, (1, 0, 1))
    coarse = levels[number + 1]
    height = 2 * coarse.rows
    hold = pairs.at[:, 0:height]
    below = restricted(field, source, hold, 0, level.size, level.size, level.shape, 16)
    refs[number + 1][0][...] = below
    solve_whole(levels, refs, pairs, number + 1)
    count = coarse.shape[0]
    solved = refs[number + 1][1][1 : 1 + count]
    column, target = iota((LANES, LANES), 0), iota((LANES, LANES), 1)
    spread = jnp.where(target // 2 == column, 1.0, 0.0).astype(F32)
    flat = dot(solved.reshape(count * coarse.rows, LANES), spread)
    flat = flat.reshape(count, coarse.rows, LANES)
    pairs[0:count, pl.ds(0, coarse.rows, stride=2), :] = flat
    pairs[0:count, pl.ds(1, coarse.rows, stride=2), :] = flat
    for plane in range(planes):
        field[plane + 1] = field[plane + 1] + pairs[plane // 2, 0:rows]
    sweeps(field, source, masks, keep, level.size, level.shape, 16, (0, 1, 0, 1))


def kernel(splits, levels, counts, density, potential, *refs):
    place = tuple(lax.axis_index(axis) for axis in AXES)
    total = counts[0] * counts[1] * counts[2]
    me = (place[0] * counts[1] + place[1]) * counts[2] + place[2]
    refs = list(refs)

    def take(number):
        taken = refs[:number]
        del refs[:number]
        return taken

    parts = []
    for level in splits:
        source, field, mask = take(3)
        of_source = Exchange(level, place, source, 0, take(8))
        of_field = Exchange(level, place, field, 1, take(8))
        parts.append((source, field, mask, of_source, of_field))
    whole_refs = [take(2) for _ in levels]
    pairs, spreads, own, slots, sent, got = take(6)

    def peer(number):
        other = lax.rem(me + number, total)
        inner = counts[1] * counts[2]
        return (lax.div(other, inner), lax.rem(lax.div(other, counts[2]), counts[1]), lax.rem(other, counts[2])), other

    barrier = pltpu.get_barrier_semaphore()

    def greet(number, carry):
        pl.semaphore_signal(
            barrier, inc=1, device_id=peer(number)[0], device_id_type=pl.DeviceIdType.MESH
        )
        return carry

    lax.fori_loop(1, total, greet, 0)

    first = splits[0]
    parts[0][0][
        first.margins[0] : first.margins[0] + first.block[0], 0 : first.block[1], 0 : first.block[2]
    ] = density[...]
    pl.semaphore_wait(barrier, total - 1)

    parts[0][3].start_xy()

    for level, (source, field, mask, of_source, of_field) in zip(splits, parts):
        plane = (level.rows, level.lanes)
        inside = None
        for dim in (1, 2):
            index = iota(plane, dim - 1)
            size = level.rows if dim == 1 else level.lanes
            margin, length = level.margins[dim], level.block[dim]
            used = (index < length + margin) | (index >= size - margin)
            spot = local_of(index, length, margin, size) + place[dim] * length
            used = used & (spot >= 0) & (spot < length * counts[dim])
            inside = used if inside is None else inside & used
        parity = (iota(plane, 0) + iota(plane, 1)) % 2
        for colour in range(2):
            mask[colour] = jnp.where(inside & (parity == colour), 1, 0)

    def keep_of(level):
        def keep(plane):
            spot = place[0] * level.block[0] + plane - level.margins[0]
            return jnp.where((spot >= 0) & (spot < level.block[0] * counts[0]), 1, 0)

        return keep

    def masks_of(mask):
        def masks(which, keep):
            return (mask[which] & keep) != 0

        return masks

    edges = [level.margins[0] for level in splits]
    before = [tuple(edge - reach for reach in (3, 2, 1)) for edge in edges]
    final = (0, splits[0].margins[0] // 2)
    after = [
        tuple(edge - reach - last for reach in (3, 2, 1, 0)) for edge, last in zip(edges, final)
    ]
    before[0] = tuple(skip - skip % 2 for skip in before[0])
    after[0] = tuple(skip - skip % 2 for skip in after[0])

    def descend(number):
        level = splits[number]
        source, field, mask, of_source, _ = parts[number]
        masks, keep = masks_of(mask), keep_of(level)
        first_half(field, source, masks, keep, level.shape, 20)
        sweeps(field, source, masks, keep, None, level.shape, 26, (1, 0, 1), before[number])
        height = 2 * up_to(level.block[1] // 2, 8)
        return restricted(
            field, source, pairs.at[:, 0:height], level.margins[0], level.block, None, level.shape, 16
        )

    def ascend(number, coarse_plane, rows_to, lanes_to, reach):
        level = splits[number]
        source, field, mask, _, _ = parts[number]
        masks, keep = masks_of(mask), keep_of(level)
        for spot in range(reach):
            spreads[spot] = dot_rows(rows_to, coarse_plane(spot))
        flat = dot(spreads[0:reach].reshape(reach * level.rows, LANES), lanes_to)
        flat = flat.reshape(reach, level.rows, level.lanes)
        for plane in range(level.planes):
            added = jnp.where(keep(plane) != 0, flat[plane // 2], 0.0)
            field[plane + 1] = field[plane + 1] + added
        sweeps(field, source, masks, keep, None, level.shape, 26, (0, 1, 0, 1), after[number])

    top, next_ = splits
    top_parts, next_parts = parts
    top_parts[3].finish_xy()
    top_parts[3].start_z()
    top_parts[3].finish_z()
    below = descend(0)
    next_parts[0][
        next_.margins[0] : next_.margins[0] + next_.block[0], 0 : next_.block[1], 0:LANES
    ] = below
    next_parts[3].start_xy()
    top_parts[4].start_xy()
    next_parts[3].finish_xy()
    next_parts[3].start_z()
    next_parts[3].finish_z()
    below = descend(1)

    length = tuple(size // 2 for size in next_.block)
    per = LANES // length[2]
    packed = jnp.zeros((8, LANES), F32)
    for plane in range(length[0]):
        moved = below[plane]
        if plane // per:
            moved = pltpu.roll(moved, length[1] * (plane // per), 0)
        if plane % per:
            moved = pltpu.roll(moved, length[2] * (plane % per), 1)
        packed = packed + moved
    own[...] = packed
    slots[me] = packed

    def send(number):
        target, other = peer(number)
        return pltpu.make_async_remote_copy(
            src_ref=own,
            dst_ref=slots.at[me],
            send_sem=sent.at[other],
            recv_sem=got.at[me],
            device_id=target,
            device_id_type=pl.DeviceIdType.MESH,
        )

    def start_send(number, carry):
        send(number).start()
        return carry

    lax.fori_loop(1, total, start_send, 0)
    next_parts[4].start_xy()
    top_parts[4].finish_xy()
    top_parts[4].start_z()
    next_parts[4].finish_xy()
    next_parts[4].start_z()

    def finish_send(number, carry):
        target, other = peer(number)
        copy = pltpu.make_async_remote_copy(
            src_ref=own,
            dst_ref=slots.at[other],
            send_sem=sent.at[other],
            recv_sem=got.at[other],
            device_id=target,
            device_id_type=pl.DeviceIdType.MESH,
        )
        copy.wait_recv()
        copy.wait_send()
        return carry

    lax.fori_loop(1, total, finish_send, 0)

    coarse_source, coarse_field = whole_refs[0]
    lane = iota((8, LANES), 1)

    def place_x(which, carry):
        for second in range(counts[1]):
            base = (which * counts[1] + second) * counts[2]
            tiles = [slots[base + third] for third in range(counts[2])]
            for spot in range(per):
                value = jnp.zeros((8, LANES), F32)
                for third in range(counts[2]):
                    shift = (length[2] * (third - spot)) % LANES
                    moved = pltpu.roll(tiles[third], shift, 1) if shift else tiles[third]
                    value = jnp.where(lane // length[2] == third, moved, value)
                for group in range(8 // length[1]):
                    plane = which * length[0] + group * per + spot
                    coarse_source[plane, second * length[1] : (second + 1) * length[1], :] = value[
                        group * length[1] : (group + 1) * length[1]
                    ]
        return carry

    lax.fori_loop(0, counts[0], place_x, 0)
    solve_whole(levels, whole_refs, pairs, 0)

    def one_hot(shape, dim, fine, fine_length, fine_margin, origin, wrap):
        index = iota(shape, dim)
        spot = local_of(index, fine_length, fine_margin, fine)
        cell = jnp.where(spot >= 0, lax.div(spot, 2), -lax.div(1 - spot, 2)) + origin
        if wrap is not None:
            cell = jnp.where(cell < 0, cell + wrap, cell)
        used = (index < fine_length + fine_margin) | (index >= fine - fine_margin)
        return jnp.where((iota(shape, 1 - dim) == cell) & used, 1.0, 0.0).astype(F32)

    coarse = levels[0]
    rows_to = one_hot(
        (next_.rows, coarse.rows), 0, next_.rows, next_.block[1], next_.margins[1],
        place[1] * length[1], None,
    )
    lanes_to = one_hot(
        (LANES, next_.lanes), 1, next_.lanes, next_.block[2], next_.margins[2],
        place[2] * length[2], None,
    )
    reach = next_.planes // 2

    def plane_of_whole(spot):
        plane = place[0] * length[0] + spot - next_.margins[0] // 2
        return coarse_field[1 + jnp.clip(plane, 0, coarse.shape[0] - 1)]

    next_parts[4].finish_z()
    ascend(1, plane_of_whole, rows_to, lanes_to, reach)

    rows_to = one_hot(
        (top.rows, next_.rows), 0, top.rows, top.block[1], top.margins[1], 0, next_.rows
    )
    lanes_to = one_hot(
        (LANES, top.lanes), 1, top.lanes, top.block[2], top.margins[2], 0, next_.lanes
    )
    shift = next_.margins[0] - top.margins[0] // 2
    top_parts[4].finish_z()
    ascend(0, lambda spot: next_parts[1][1 + spot + shift], rows_to, lanes_to, top.planes // 2)
    potential[...] = top_parts[1][
        1 + top.margins[0] : 1 + top.margins[0] + top.block[0], 0 : top.block[1], 0 : top.block[2]
    ]
    for part in parts:
        part[3].drain()
        part[4].drain()


def flat_scratch(entries):
    out = []
    for entry in entries:
        out.extend(flat_scratch(entry) if isinstance(entry, (list, tuple)) else [entry])
    return out


def on_device(counts, density):
    block = density.shape
    half_block = tuple(size // 2 for size in block)
    splits = [
        Split(block, (4, 4, 4), counts),
        Split(half_block, (6, 8, 8), counts),
    ]
    size = tuple(block[which] * counts[which] // 4 for which in range(3))
    levels = []
    for number in range(2, LEVELS):
        levels.append(Whole(size))
        size = tuple(max(part // 2, 1) for part in size)
    total = counts[0] * counts[1] * counts[2]
    pair_planes = max(block[0] // 2, levels[0].shape[0])
    pair_rows = max(block[1], levels[0].rows, 16)
    scratch = [level.scratch() for level in splits] + [level.scratch() for level in levels]
    scratch = flat_scratch(scratch) + [
        pltpu.VMEM((pair_planes, pair_rows, LANES), F32),
        pltpu.VMEM((max(level.planes // 2 for level in splits), splits[0].rows, LANES), F32),
        pltpu.VMEM((8, LANES), F32),
        pltpu.VMEM((total, 8, LANES), F32),
        pltpu.SemaphoreType.DMA((total,)),
        pltpu.SemaphoreType.DMA((total,)),
    ]
    return pl.pallas_call(
        functools.partial(kernel, splits, levels, counts),
        out_shape=jax.ShapeDtypeStruct(block, F32),
        in_specs=[pl.BlockSpec(memory_space=pltpu.VMEM)],
        out_specs=pl.BlockSpec(memory_space=pltpu.VMEM),
        scratch_shapes=scratch,
        compiler_params=pltpu.CompilerParams(
            collective_id=0, has_side_effects=True, vmem_limit_bytes=48 * 1024 * 1024
        ),
    )(density)


def solution(mesh):
    counts = tuple(mesh.shape[axis] for axis in AXES)
    return jax.shard_map(
        functools.partial(on_device, counts),
        mesh=mesh,
        in_specs=(P("gx", "gy", "gz"),),
        out_specs=P("gx", "gy", "gz"),
        check_vma=False,
    )
```

profile of v0, /device:TPU:0, one launch (start us, length us, event | category | flops | bytes accessed | tf_op | source)
XLA Modules:
  0.0 40.5 jit_solution(3626255930020597299)
XLA Ops:
  0.0 0.0 copy-start
  0.0 0.9 %copy-done = f32[32,16,128]{2,1,0:T(8,128)S(1)} copy-done((f32[32,16,128]{2,1,0:T(8,128)S(1)}, f32[32,16,128]{2,1,0:T(8,128)}, u32[]{:S(2)}) %copy-start) | copy-done | bytes 262168
  1.0 38.8 %shard_map.17 = f32[32,16,128]{2,1,0:T(8,128)S(1)} custom-call(f32[32,16,128]{2,1,0:T(8,128)S(1)} %copy-done), custom_call_target="tpu_custom_call" | custom-call | tf_op jit(solution)/shard_map/pallas_call | solution.py:654
  39.8 0.7 %copy.3 = f32[32,16,128]{2,1,0:T(8,128)} copy(f32[32,16,128]{2,1,0:T(8,128)S(1)} %shard_map.17) | data formatting | bytes 524288
Async XLA Ops:
  0.0 0.9 %copy-start = (f32[32,16,128]{2,1,0:T(8,128)S(1)}, f32[32,16,128]{2,1,0:T(8,128)}, u32[]{:S(2)}) copy-start(f32[32,16,128]{2,1,0:T(8,128)} %density.1) | copy-start | bytes 786436
where the time goes:
time: 40.7 us; the launch traced here: 40.5 us
  Pallas kernels  38.8 us (95%)
  local copies, waits for them, and re-layouts  1.65 us (4%)
    pallas_call x1, Pallas kernels, on_device(): pl.pallas_call(functools.partial(kernel, splits, levels, counts), out_sha...  38.8 us
    unnamed x3, local copies, waits for them, and re-layouts  1.65 us

commit v1 on v0

v1 whole, which is shorter than its diff:
```python
import functools

import jax
import jax.numpy as jnp
import numpy as np
from jax import lax
from jax.experimental import pallas as pl
from jax.experimental.pallas import tpu as pltpu
from jax.sharding import PartitionSpec as P

LEVELS = 7
CSWEEPS = 4
DENSE = 512
rsd_beta = 0.5
centre = 4.0 + 2.0 * (1.0 + rsd_beta)
along = 1.0 + rsd_beta
inverse = 1.0 / centre
F32 = jnp.float32
BF16 = jnp.bfloat16
LANES = 128
AXES = ("gx", "gy", "gz")
MESH = pl.DeviceIdType.MESH
DIRECTIONS = [
    (dx, dy, dz) for dx in (-1, 0, 1) for dy in (-1, 0, 1) for dz in (-1, 0, 1) if (dx, dy, dz) != (0, 0, 0)
]
STEPS_XY = [(dx, dy) for dx in (-1, 0, 1) for dy in (-1, 0, 1) if (dx, dy) != (0, 0)]


def up_to(value, unit):
    return -(-value // unit) * unit


def iota(shape, dim):
    return lax.broadcasted_iota(jnp.int32, shape, dim)


def pieces(value):
    high = value.astype(BF16)
    rest = value - high.astype(F32)
    middle = rest.astype(BF16)
    return high, middle, (rest - middle.astype(F32)).astype(BF16)


def product(left, right):
    return jnp.dot(left, right, preferred_element_type=F32)


def dot(value, chosen):
    chosen = chosen.astype(BF16)
    parts = [product(part, chosen) for part in pieces(value)]
    return parts[0] + (parts[1] + parts[2])


def local_of(index, length, margin, total):
    return jnp.where(index < total - margin, index, index - total)


def half_down(value):
    return jnp.where(value >= 0, lax.div(value, 2), -lax.div(1 - value, 2))


def parity_of(rows, lanes):
    return (iota((rows, lanes), 0) + iota((rows, lanes), 1)) % 2 == 0


def beside(below, here, above, even, colour, edge):
    rows, lanes = here.shape
    down, up = pltpu.roll(here, 1, 0), pltpu.roll(here, rows - 1, 0)
    left, right = pltpu.roll(here, 1, 1), pltpu.roll(here, lanes - 1, 1)
    if edge is not None:
        if edge[0] == rows:
            row = iota(here.shape, 0)
            down = jnp.where(row == 0, 0.0, down)
            up = jnp.where(row == rows - 1, 0.0, up)
        if edge[1] == lanes:
            lane = iota(here.shape, 1)
            left = jnp.where(lane == 0, 0.0, left)
            right = jnp.where(lane == lanes - 1, 0.0, right)
    other = jnp.where(even, below, above) if colour == 0 else jnp.where(even, above, below)
    return (here + other) + (down + up) + along * (left + right)


class Grid:
    def __init__(self, block, margins, edge=False):
        self.block, self.margins = block, margins
        self.inner = block[0] // 2
        self.count = self.inner + 2 * margins[0]
        self.rows = up_to(block[1] + 2 * margins[1], 8)
        self.lanes = up_to(block[2] + 2 * margins[2], LANES)
        self.edge = (block[1], block[2]) if edge else None

    def scratch(self, name):
        field = (self.count + 2, self.rows, self.lanes)
        source = (self.count, self.rows, self.lanes)
        return {
            name + "R": pltpu.VMEM(field, F32),
            name + "B": pltpu.VMEM(field, F32),
            name + "f": pltpu.VMEM(source, F32),
            name + "g": pltpu.VMEM(source, F32),
            name + "m": pltpu.VMEM((3, self.rows, self.lanes), F32),
        }

    def zone(self, number):
        if number < self.margins[0]:
            return 0
        return 2 if number >= self.count - self.margins[0] else 1

    def guard(self, s, name):
        empty = jnp.zeros((self.rows, self.lanes), F32)
        for key in "RB":
            s[name + key][0] = empty
            s[name + key][self.count + 1] = empty

    def masks(self, s, name, place, counts):
        inside = None
        shape = (self.rows, self.lanes)
        for dim in (1, 2):
            index = iota(shape, dim - 1)
            size = shape[dim - 1]
            margin, length = self.margins[dim], self.block[dim]
            used = (index < length + margin) | (index >= size - margin)
            spot = local_of(index, length, margin, size) + place[dim] * length
            used = used & (spot >= 0) & (spot < length * counts[dim])
            inside = used if inside is None else inside & used
        value = jnp.where(inside, inverse, 0.0).astype(F32)
        s[name + "m"][1] = value
        if self.margins[0]:
            low = jnp.where(place[0] > 0, 1.0, 0.0).astype(F32)
            high = jnp.where(place[0] < counts[0] - 1, 1.0, 0.0).astype(F32)
            s[name + "m"][0] = value * low
            s[name + "m"][2] = value * high

    def first(self, s, name, begin, end):
        for number in range(begin, end):
            s[name + "R"][number + 1] = s[name + "f"][number] * s[name + "m"][self.zone(number)]

    def totals(self, other, even, colour, begin, end):
        before, here = other[begin], other[begin + 1]
        for number in range(begin, end):
            after = other[number + 2]
            yield number, beside(before, here, after, even, colour, self.edge)
            before, here = here, after

    def half(self, s, name, colour, even, begin, end):
        target, other = (s[name + "R"], s[name + "B"]) if colour == 0 else (s[name + "B"], s[name + "R"])
        source = s[name + ("f" if colour == 0 else "g")]
        for number, total in self.totals(other, even, colour, begin, end):
            target[number + 1] = (source[number] + total) * s[name + "m"][self.zone(number)]

    def residue(self, s, name, even, begin, end):
        for number, total in self.totals(s[name + "B"], even, 0, begin, end):
            yield number, s[name + "f"][number] - centre * s[name + "R"][number + 1] + total

    def planes(self, s, name, even, plane):
        red, black = s[name + "R"][plane // 2 + 1], s[name + "B"][plane // 2 + 1]
        return jnp.where(even, red, black) if plane % 2 == 0 else jnp.where(even, black, red)


def exists(place, steps, counts):
    found = None
    for which in range(3):
        if steps[which] == 0:
            continue
        other = place[which] + steps[which]
        here = (other >= 0) & (other < counts[which])
        found = here if found is None else found & here
    return found


def device(place, steps):
    return tuple(place[which] + steps[which] for which in range(3))


def back(steps):
    return tuple(-step for step in steps)


class Exchange:
    def __init__(self, level, place, counts, array, refs):
        self.level, self.place, self.counts, self.array = level, place, counts, array
        self.block = (level.inner, level.block[1], level.block[2])
        self.margins = level.margins
        self.per = LANES // level.margins[2]
        self.packs = -(-level.count // self.per)
        (self.stage_x, self.land_x, self.land_y, self.stage_y) = refs[:4]
        (self.stage_z, self.land_z, self.sent, self.got) = refs[4:]

    @staticmethod
    def scratch(level, name):
        per = LANES // level.margins[2]
        packs = -(-level.count // per)
        margin, rows = level.margins, level.block[1]
        shapes = [
            (2, margin[0], rows, LANES),
            (2, margin[0], rows, LANES),
            (2, level.count, margin[1], LANES),
            (2, level.inner, margin[1], LANES),
            (2, packs, level.rows, LANES),
            (2, packs, level.rows, LANES),
        ]
        out = {name + str(number): pltpu.VMEM(shape, F32) for number, shape in enumerate(shapes)}
        out[name + "6"] = pltpu.SemaphoreType.DMA((10,))
        out[name + "7"] = pltpu.SemaphoreType.DMA((10,))
        return out

    def xy(self, number):
        dx, dy = STEPS_XY[number]
        margin, length = self.margins[0], self.block[0]
        place = {1: 0, 0: margin, -1: margin + length}[dx]
        count = length if dx == 0 else margin
        origin = length - margin if dx == 1 else 0
        if dy == 0:
            source = self.stage_x.at[(dx + 1) // 2]
            target = self.land_x.at[(dx + 1) // 2]
        else:
            source = self.stage_y.at[(dy + 1) // 2, pl.ds(origin, count)]
            target = self.land_y.at[(dy + 1) // 2, pl.ds(place, count)]
        return (dx, dy, 0), (place, count), pltpu.make_async_remote_copy(
            src_ref=source,
            dst_ref=target,
            send_sem=self.sent.at[number],
            recv_sem=self.got.at[number],
            device_id=device(self.place, (dx, dy, 0)),
            device_id_type=MESH,
        )

    def start_xy(self):
        array, margin = self.array, self.margins
        low = 1 + margin[0]
        length, rows = self.block[0], self.block[1]
        self.stage_y[0] = array[low : low + length, 0 : margin[1], 0:LANES]
        self.stage_y[1] = array[low : low + length, rows - margin[1] : rows, 0:LANES]
        self.stage_x[0] = array[low : low + margin[0], 0:rows, 0:LANES]
        self.stage_x[1] = array[low + length - margin[0] : low + length, 0:rows, 0:LANES]
        for number in range(8):
            steps, _, copy = self.xy(number)

            @pl.when(exists(self.place, steps, self.counts))
            def _():
                copy.start()

    def finish_xy(self):
        array, rows, margin = self.array, self.block[1], self.margins[1]
        for number in range(8):
            steps, (place, count), copy = self.xy(number)

            @pl.when(exists(self.place, back(steps), self.counts))
            def _():
                copy.wait_recv()
                low = 1 + place
                if steps[1] == 0:
                    array[low : low + count, 0:rows, 0:LANES] = self.land_x[(steps[0] + 1) // 2]
                else:
                    first = self.level.rows - margin if steps[1] == 1 else rows
                    side = (steps[1] + 1) // 2
                    array[low : low + count, first : first + margin, 0:LANES] = self.land_y[
                        side, place : place + count
                    ]

    def z(self, side):
        return pltpu.make_async_remote_copy(
            src_ref=self.stage_z.at[side],
            dst_ref=self.land_z.at[side],
            send_sem=self.sent.at[8 + side],
            recv_sem=self.got.at[8 + side],
            device_id=device(self.place, (0, 0, 2 * side - 1)),
            device_id_type=MESH,
        )

    def start_z(self):
        level, array = self.level, self.array
        margin, length = self.margins[2], self.block[2]
        lane = iota((level.rows, LANES), 1)
        for side in range(2):
            first = length - margin if side == 1 else 0
            for pack in range(self.packs):
                total = jnp.zeros((level.rows, LANES), F32)
                for number in range(min(self.per, level.count - pack * self.per)):
                    plane = array[1 + pack * self.per + number, :, 0:LANES]
                    moved = pltpu.roll(plane, (number * margin - first) % LANES, 1)
                    total = jnp.where(lane // margin == number, moved, total)
                self.stage_z[side, pack] = total
        for side in range(2):
            @pl.when(exists(self.place, (0, 0, 2 * side - 1), self.counts))
            def _():
                self.z(side).start()

    def finish_z(self):
        level, array = self.level, self.array
        margin, length = self.margins[2], self.block[2]
        base = level.lanes - LANES
        lane = iota((level.rows, LANES), 1)
        have = []
        for side in range(2):
            there = exists(self.place, (0, 0, 1 - 2 * side), self.counts)
            have.append(there)

            @pl.when(there)
            def _():
                self.z(side).wait_recv()

        above = length - base
        take_above = (lane >= above) & (lane < above + margin) & have[0]
        take_below = (lane >= LANES - margin) & have[1]
        for pack in range(self.packs):
            from_above, from_below = self.land_z[0, pack], self.land_z[1, pack]
            for number in range(min(self.per, level.count - pack * self.per)):
                plane = 1 + pack * self.per + number
                high = pltpu.roll(from_above, (above - number * margin) % LANES, 1)
                low = pltpu.roll(from_below, (LANES - margin - number * margin) % LANES, 1)
                value = array[plane, :, base : level.lanes]
                value = jnp.where(take_above, high, value)
                array[plane, :, base : level.lanes] = jnp.where(take_below, low, value)

    def drain(self):
        for number in range(8):
            steps, _, copy = self.xy(number)

            @pl.when(exists(self.place, steps, self.counts))
            def _():
                copy.wait_send()

        for side in range(2):
            @pl.when(exists(self.place, (0, 0, 2 * side - 1), self.counts))
            def _():
                self.z(side).wait_send()


class Plan:
    def __init__(self, block, counts):
        self.counts, self.block = counts, block
        self.total = counts[0] * counts[1] * counts[2]
        self.block1 = tuple(size // 2 for size in block)
        self.block2 = tuple(size // 4 for size in block)
        self.top = Grid(block, (2, 4, 4))
        self.wide = Grid(block, (4, 8, 8))
        self.next = Grid(self.block1, (3, 8, 8))
        self.width = up_to(block[2], LANES)
        self.tiles = self.top.lanes // LANES
        self.count = self.top.count
        self.high = self.block1[1] + 8
        self.per = LANES // self.block1[2]
        self.side = 8 // self.per
        self.middle = (self.count - 16) // self.per
        self.vectors = 2 * self.side + self.middle + 1
        self.packs = 1 + (self.count > 16)
        self.far_packs = block[0] // 16
        assert block[0] % 16 == 0 and self.block1[1] % 8 == 0 and self.block2[2] <= LANES
        assert self.next.lanes == LANES and (self.count - 16) % self.per == 0 and 64 % self.block1[2] == 0
        self.levels = []
        size = tuple(block[which] * counts[which] // 4 for which in range(3))
        number = 2
        while size[0] * size[1] * size[2] > DENSE:
            self.levels.append(Grid(size, (0, 0, 0), edge=True))
            assert self.levels[-1].lanes == LANES
            size = tuple(part // 2 for part in size)
            number += 1
        self.dense, self.dense_level = size, number

    def message(self, steps):
        dx, dy, dz = steps
        if dz == 0:
            begin, length = {0: (0, self.vectors), -1: (0, self.side + 1), 1: (self.side, self.side + 1)}[dx]
            if dy == 0:
                return ("part_t", (pl.ds(begin, length),), (length, self.high, LANES))
            return ("part_y", ((dy + 1) // 2, pl.ds(begin, length)), (length, 8, LANES))
        length = self.packs if dx == 0 else 1
        if dy == 0:
            return ("part_z", ((dz + 1) // 2, pl.ds(0, length)), (length, self.high, LANES))
        return (
            "part_zy", ((dz + 1) // 2, (dy + 1) // 2, pl.ds(0, length)), (length, 8, LANES),
        )

    def scratch(self):
        block = self.block
        s = {}
        for name, grid in (("top", self.top), ("wide", self.wide), ("next", self.next)):
            s.update(grid.scratch(name))
        for number, grid in enumerate(self.levels):
            s.update(grid.scratch(f"level{number}"))
        s["own"] = pltpu.VMEM((block[0], block[1], self.width), F32)
        if block[2] != self.width:
            s["raw"] = pltpu.VMEM(block, F32)
        s["field"] = pltpu.VMEM((block[0] + 16, block[1] + 16, self.wide.lanes), F32)
        for tile in range(self.tiles):
            s[f"rows{tile}"] = pltpu.VMEM((self.count, block[1] + 16, LANES), F32)
        s["part"] = pltpu.VMEM((self.count, self.high, LANES), F32)
        s["part_t"] = pltpu.VMEM((self.vectors, self.high, LANES), F32)
        s["part_y"] = pltpu.VMEM((2, self.vectors, 8, LANES), F32)
        s["part_z"] = pltpu.VMEM((2, self.packs, self.high, LANES), F32)
        s["part_zy"] = pltpu.VMEM((2, 2, self.packs, 8, LANES), F32)
        for number, steps in enumerate(DIRECTIONS):
            s[f"land{number}"] = pltpu.VMEM(self.message(steps)[2], F32)
        wide_rows = self.block1[1] + 16
        for dx in (-1, 0, 1):
            length = self.vectors if dx == 0 else self.side + 1
            packs = self.packs if dx == 0 else 1
            s[f"sum{dx}"] = pltpu.VMEM((length, wide_rows, LANES), F32)
            s[f"sumz{dx}"] = pltpu.VMEM((2, packs, wide_rows, LANES), F32)
        s["far"] = pltpu.VMEM((2, self.far_packs, block[1], LANES), F32)
        s["far_land"] = pltpu.VMEM((2, self.far_packs + 2, block[1] + 16, LANES), F32)
        s.update(Exchange.scratch(self.next, "swap"))
        first = self.levels[0]
        coarse = [first] + self.levels[1:]
        s["pairs"] = pltpu.VMEM((max(g.block[0] for g in coarse + [self.next]), 2 * up_to(first.rows, 16), LANES), F32)
        s["solved"] = pltpu.VMEM((first.block[0] + 6, first.rows, LANES), F32)
        s["spread"] = pltpu.VMEM((self.next.count, 2 * first.rows + 32, LANES), F32)
        s["whole"] = pltpu.VMEM((first.block[0], first.rows, LANES), F32)
        s["mine"] = pltpu.VMEM((8, LANES), F32)
        s["slots"] = pltpu.VMEM((self.total, 8, LANES), F32)
        size = self.dense[0] * self.dense[1] * self.dense[2]
        s["matrix"] = pltpu.VMEM((3, size, size), BF16)
        for name, number in (
            ("sent", self.total), ("got", self.total), ("part_sent", 26), ("part_got", 26),
            ("far_sent", 26), ("far_got", 26), ("loads", 3),
        ):
            s["sem_" + name] = pltpu.SemaphoreType.DMA((number,))
        return s


def weights(shape, found, value):
    return jnp.where(found, value, 0.0).astype(F32).reshape(shape)


def pair_sums(s, height, count):
    even = s[0:count, pl.ds(0, height // 2, stride=2), :]
    return even + s[0:count, pl.ds(1, height // 2, stride=2), :]


def send_part(plan, s, place, number):
    steps = DIRECTIONS[number]
    name, index, _ = plan.message(steps)
    return pltpu.make_async_remote_copy(
        src_ref=s[name].at[index],
        dst_ref=s[f"land{number}"],
        send_sem=s["sem_part_sent"].at[number],
        recv_sem=s["sem_part_got"].at[number],
        device_id=device(place, steps),
        device_id_type=MESH,
    )


def send_far(plan, s, place, number):
    dx, dy, dz = steps = DIRECTIONS[number]
    block = plan.block
    rows = {0: (0, block[1], 0), 1: (block[1] - 8, 8, block[1] + 8), -1: (0, 8, block[1])}[dy]
    if dz == 0:
        planes = {0: (0, block[0], 8), 1: (block[0] - 8, 8, 0), -1: (0, 8, block[0] + 8)}[dx]
        source = s["own"].at[pl.ds(planes[0], planes[1]), pl.ds(rows[0], rows[1]), :]
        target = s["field"].at[pl.ds(planes[2], planes[1]), pl.ds(rows[2], rows[1]), pl.ds(0, plan.width)]
    else:
        side, last = (dz + 1) // 2, plan.far_packs - 1
        packs = {0: (0, last + 1, 1), 1: (last, 1, 0), -1: (0, 1, last + 2)}[dx]
        source = s["far"].at[side, pl.ds(packs[0], packs[1]), pl.ds(rows[0], rows[1]), :]
        target = s["far_land"].at[side, pl.ds(packs[2], packs[1]), pl.ds(rows[2], rows[1]), :]
    return pltpu.make_async_remote_copy(
        src_ref=source,
        dst_ref=target,
        send_sem=s["sem_far_sent"].at[number],
        recv_sem=s["sem_far_got"].at[number],
        device_id=device(place, steps),
        device_id_type=MESH,
    )


def each(place, counts, send, action, reverse=False):
    for number, steps in enumerate(DIRECTIONS):
        @pl.when(exists(place, back(steps) if reverse else steps, counts))
        def _():
            getattr(send(number), action)()


def pack_part(plan, s):
    count, per, side, middle, rows = plan.count, plan.per, plan.side, plan.middle, plan.block1[1]
    length = plan.block1[2]
    part = s["part"]
    shape = (plan.high, LANES)
    lane = iota(shape, 1)
    sub = iota((8, LANES), 0)

    def pair_y(value):
        edge = value[rows:]
        minus = jnp.where(sub >= 6, edge, value[:8])
        return minus, jnp.where(sub < 2, edge, value[rows - 8 : rows])

    groups = [(0, 0, side), (side + 1, count - 8, side), (2 * side + 1, 8, middle)]
    for index, first, number in groups:
        for spot in range(number):
            value = part[first + spot]
            for which in range(1, per):
                moved = pltpu.roll(part[first + spot + which * number], which * length, 1)
                value = jnp.where(lane // length == which, moved, value)
            s["part_t"][index + spot] = value
            minus, plus = pair_y(value)
            s["part_y"][0, index + spot] = minus
            s["part_y"][1, index + spot] = plus
    value = jnp.zeros(shape, F32)
    couple = lane // 2
    for number in range(count):
        low = pltpu.roll(part[number], 2 * number, 1)
        high = low if length == 64 else pltpu.roll(part[number], 64 - length + 2 * number, 1)
        value = jnp.where(couple == ((126 + 2 * number) % LANES) // 2, low, value)
        value = jnp.where(couple == 32 + number, high, value)
    s["part_t"][side] = value
    minus, plus = pair_y(value)
    s["part_y"][0, side] = minus
    s["part_y"][1, side] = plus
    for which in range(2):
        begin = LANES - 2 if which == 0 else length - 6
        for pack in range(plan.packs):
            value = jnp.zeros(shape, F32)
            planes = list(range(8)) + list(range(count - 8, count)) if pack == 0 else list(range(8, count - 8))
            for slot, number in enumerate(planes):
                moved = pltpu.roll(part[number], (8 * slot - begin) % LANES, 1)
                value = jnp.where(lane // 8 == slot, moved, value)
            s["part_z"][which, pack] = value
            minus, plus = pair_y(value)
            s["part_zy"][which, 0, pack] = minus
            s["part_zy"][which, 1, pack] = plus


def gather_part(plan, s):
    side, count, rows, per, length = plan.side, plan.count, plan.block1[1], plan.per, plan.block1[2]
    sub = iota((8, LANES), 0)
    land = {steps: s[f"land{number}"] for number, steps in enumerate(DIRECTIONS)}

    def assembled(own, plus, minus):
        edge = own[rows:]
        tiles = [own[8 * number : 8 * number + 8] for number in range(rows // 8)]
        tiles[0] = tiles[0] + jnp.where(sub < 2, minus, 0.0)
        tiles[-1] = tiles[-1] + jnp.where(sub >= 6, plus, 0.0)
        tiles.append(jnp.where(sub < 6, plus, 0.0) + jnp.where(sub < 2, edge, 0.0))
        tiles.append(jnp.where(sub >= 2, minus, 0.0) + jnp.where(sub >= 6, edge, 0.0))
        return jnp.concatenate(tiles, axis=0)

    for dx in (-1, 0, 1):
        own = s["part_t"] if dx == 0 else land[(dx, 0, 0)]
        for index in range(own.shape[0]):
            s[f"sum{dx}"][index] = assembled(own[index], land[(dx, -1, 0)][index], land[(dx, 1, 0)][index])
        for which in range(2):
            dz = 2 * which - 1
            for pack in range(land[(dx, 0, dz)].shape[0]):
                s[f"sumz{dx}"][which, pack] = assembled(
                    land[(dx, 0, dz)][pack], land[(dx, -1, dz)][pack], land[(dx, 1, dz)][pack]
                )

    shape = (rows + 16, LANES)
    lane = iota(shape, 1)
    at_low, at_high = lane >= LANES - 2, (lane == length) | (lane == length + 1)
    inner = lane < length
    above = (lane >= length - 2) & (lane < length + 6)
    below = (lane >= LANES - 6) | (lane < 2)
    even = parity_of(*shape)

    def turned(value, shift):
        shift = shift % LANES
        return pltpu.roll(value, shift, 1) if shift else value

    def plane_of(dx, number):
        if number < 8:
            index, slots, size, first = number, number, side, 0
            base = 0
        elif number >= count - 8:
            index, slots, size, first = number - (count - 8), 8 + number - (count - 8), side, count - 8
            base = side + 1
        else:
            index, slots, size, first = number - 8, number - 8, plan.middle, 8
            base = 2 * side + 1
        pack = 0 if number < 8 or number >= count - 8 else 1
        extra = side
        if dx == -1:
            base, extra = 0, side
        if dx == 1:
            base, extra = 1, 0
        total = s[f"sum{dx}"]
        main = turned(total[base + index % size], -(index // size) * length)
        low = turned(total[extra], -2 * number)
        high = low if length == 64 else turned(total[extra], length - 64 - 2 * number)
        value = jnp.where(inner, main, jnp.where(at_low, low, jnp.where(at_high, high, 0.0)))
        far = s[f"sumz{dx}"]
        from_above = turned(far[0, pack], length - 2 - 8 * slots)
        from_below = turned(far[1, pack], LANES - 6 - 8 * slots)
        return value + (jnp.where(above, from_above, 0.0) + jnp.where(below, from_below, 0.0))

    def plane(number):
        spot = number - 2 * plan.next.margins[0]
        total = None
        for dx, place in ((0, spot), (-1, spot - plan.block1[0]), (1, spot + plan.block1[0])):
            index = place + 2
            allowed = {0: (0, count), -1: (0, 8), 1: (count - 8, count)}[dx]
            if allowed[0] <= index < allowed[1]:
                value = plane_of(dx, index)
                total = value if total is None else total + value
        return total

    for number in range(plan.next.count):
        first, second = plane(2 * number), plane(2 * number + 1)
        s["nextf"][number] = jnp.where(even, first, second)
        s["nextg"][number] = jnp.where(even, second, first)


def solve(plan, s, number):
    grid, name = plan.levels[number], f"level{number}"
    even = parity_of(grid.rows, LANES)
    count = grid.count
    grid.first(s, name, 0, count)
    for colour in (1, 0, 1):
        grid.half(s, name, colour, even, 0, count)
    pairs = s["pairs"]
    height = max(grid.rows, 16)
    if grid.rows < height:
        pairs[0:count, grid.rows : height] = jnp.zeros((count, height - grid.rows, LANES), F32)
    for spot, value in grid.residue(s, name, even, 0, count):
        if grid.rows > grid.block[1]:
            value = jnp.where(iota(value.shape, 0) < grid.block[1], value, 0.0)
        pairs[spot, 0 : grid.rows] = value
    flat = pair_sums(pairs, height, count).reshape(count * (height // 2), LANES)
    row, column = iota((LANES, LANES), 0), iota((LANES, LANES), 1)
    if number + 1 < len(plan.levels):
        below, under = plan.levels[number + 1], f"level{number + 1}"
        down = weights((LANES, LANES), (row // 2 == column) & (row < grid.block[2]), 0.5)
        coarse = dot(flat, down).reshape(count, height // 2, LANES)[:, : below.rows]
        same = parity_of(below.rows, LANES)
        for spot in range(below.count):
            one, two = coarse[2 * spot], coarse[2 * spot + 1]
            s[under + "f"][spot] = jnp.where(same, one, two)
            s[under + "g"][spot] = jnp.where(same, two, one)
        solve(plan, s, number + 1)
        planes = [below.planes(s, under, same, plane) for plane in range(count)]
        spread = weights((LANES, LANES), column // 2 == row, 1.0)
        flat = dot(jnp.concatenate(planes, axis=0), spread).reshape(count, below.rows, LANES)
        pairs[0:count, pl.ds(0, below.rows, stride=2), :] = flat
        pairs[0:count, pl.ds(1, below.rows, stride=2), :] = flat
        for spot in range(count):
            s[name + "B"][spot + 1] = s[name + "B"][spot + 1] + pairs[spot, 0 : grid.rows]
    else:
        nx, ny, nz = plan.dense
        size = nx * ny * nz
        tall = height // 2
        down = weights((LANES, LANES), (row // 2 == column % nz) & (row < grid.block[2]), 0.5)
        many = dot(flat, down).reshape(count, tall, LANES)
        wide = up_to(size, LANES) // LANES
        here, lane = iota((tall, LANES), 0), iota((tall, LANES), 1)
        parts = []
        for vector in range(wide):
            cell = (vector * LANES + lane) // nz
            total = jnp.zeros((tall, LANES), F32)
            for spot in range(nx):
                total = total + jnp.where((cell == spot * ny + here) & (here < ny), many[spot], 0.0)
            parts.append(total)
        left = jnp.concatenate(parts, axis=1)[:, :size]
        high, middle, low = pieces(left)
        stack = jnp.concatenate([high, middle, low], axis=0)
        matrix = s["matrix"]
        one = product(stack, matrix[0])
        two = product(stack[: 2 * tall], matrix[1])
        three = product(high, matrix[2])
        total = one[:tall] + ((one[tall : 2 * tall] + one[2 * tall :]) + ((two[:tall] + two[tall:]) + three))
        answer = jnp.sum(total, axis=0, keepdims=True)
        here, lane = iota((grid.rows, LANES), 0), iota((grid.rows, LANES), 1)
        planes = []
        for spot in range(nx):
            value = jnp.zeros((grid.rows, LANES), F32)
            for vector in range(wide):
                if (vector + 1) * LANES <= spot * ny * nz or vector * LANES >= (spot + 1) * ny * nz:
                    continue
                piece = jnp.broadcast_to(answer[:, vector * LANES : (vector + 1) * LANES], value.shape)
                cell = (vector * LANES + lane) // nz
                value = jnp.where(cell == spot * ny + here // 2, piece, value)
            planes.append(value)
        spread = weights((LANES, LANES), (column // 2 == row % nz) & (column < grid.block[2]), 1.0)
        flat = dot(jnp.concatenate(planes, axis=0), spread).reshape(count, grid.rows, LANES)
        for spot in range(count):
            s[name + "B"][spot + 1] = s[name + "B"][spot + 1] + flat[spot]
    for colour in (0, 1, 0, 1):
        grid.half(s, name, colour, even, 0, count)


def kernel(plan, names, density, dense, potential, *refs):
    s = dict(zip(names, refs))
    counts, block, total = plan.counts, plan.block, plan.total
    top, wide, next_ = plan.top, plan.wide, plan.next
    place = tuple(lax.axis_index(axis) for axis in AXES)
    me = (place[0] * counts[1] + place[1]) * counts[2] + place[2]
    padded = block[2] != plan.width

    loads = [pltpu.make_async_copy(density, s["raw" if padded else "own"], s["sem_loads"].at[0])]
    loads[0].start()
    if not padded:
        loads.append(
            pltpu.make_async_copy(
                density,
                s["field"].at[pl.ds(8, block[0]), pl.ds(0, block[1]), pl.ds(0, block[2])],
                s["sem_loads"].at[1],
            )
        )
        loads[1].start()
    fill = pltpu.make_async_copy(dense, s["matrix"], s["sem_loads"].at[2])
    fill.start()

    for number in range(26):
        ref = s[f"land{number}"]
        ref[...] = jnp.zeros(ref.shape, F32)

    def peer(number):
        other = lax.rem(me + number, total)
        inner = counts[1] * counts[2]
        return (lax.div(other, inner), lax.rem(lax.div(other, counts[2]), counts[1]), lax.rem(other, counts[2])), other

    barrier = pltpu.get_barrier_semaphore()

    def greet(number, carry):
        pl.semaphore_signal(barrier, inc=1, device_id=peer(number)[0], device_id_type=MESH)
        return carry

    lax.fori_loop(1, total, greet, 0)

    for name in ("topf", "topg", "topR", "topB"):
        s[name][...] = jnp.zeros(s[name].shape, F32)
    for name, grid in (("top", top), ("wide", wide), ("next", next_)):
        grid.guard(s, name)
        grid.masks(s, name, place, counts)
    for number, grid in enumerate(plan.levels):
        grid.guard(s, f"level{number}")
        grid.masks(s, f"level{number}", (0, 0, 0), (1, 1, 1))
    loads[0].wait()
    own = s["own"]
    if padded:
        own[...] = jnp.zeros(own.shape, F32)
        own[:, :, 0 : block[2]] = s["raw"][...]

    even_own = parity_of(block[1], plan.width)
    for number in range(top.inner):
        one, two = own[2 * number], own[2 * number + 1]
        red = jnp.where(even_own, one, two)
        spot = number + top.margins[0]
        s["topf"][spot, 0 : block[1], 0 : plan.width] = red
        s["topg"][spot, 0 : block[1], 0 : plan.width] = jnp.where(even_own, two, one)
        s["topR"][spot + 1, 0 : block[1], 0 : plan.width] = red * inverse
    even_top = parity_of(top.rows, top.lanes)
    count = top.count
    top.half(s, "top", 1, even_top, 1, count - 1)
    top.half(s, "top", 0, even_top, 1, count - 1)
    top.half(s, "top", 1, even_top, 0, count)
    for number, value in top.residue(s, "top", even_top, 0, count):
        for tile in range(plan.tiles):
            piece = value[:, tile * LANES : (tile + 1) * LANES]
            s[f"rows{tile}"][number, 0 : top.rows] = piece
            s[f"rows{tile}"][number, top.rows : top.rows + 8] = piece[block[1] :]
    flat = jnp.concatenate(
        [
            pair_sums(s[f"rows{tile}"], block[1] + 16, count).reshape(count * plan.high, LANES)
            for tile in range(plan.tiles)
        ],
        axis=1,
    )

    def fine_cell(shape, dim):
        index = iota(shape, dim)
        used = (index < block[2] + 4) | (index >= top.lanes - 4)
        cell = half_down(local_of(index, block[2], 4, top.lanes))
        return jnp.where(cell < 0, cell + LANES, cell), used

    shape = (top.lanes, LANES)
    cell, used = fine_cell(shape, 0)
    down = weights(shape, (cell == iota(shape, 1)) & used, 0.5)
    s["part"][...] = dot(flat, down).reshape(count, plan.high, LANES)
    pack_part(plan, s)

    pl.semaphore_wait(barrier, total - 1)
    part = functools.partial(send_part, plan, s, place)
    far = functools.partial(send_far, plan, s, place)
    each(place, counts, part, "start")

    lane = iota((block[1], LANES), 1)
    for side in range(2):
        begin = 0 if side == 0 else block[2] - 8
        tile = begin // LANES
        for pack in range(plan.far_packs):
            value = jnp.zeros((block[1], LANES), F32)
            for slot in range(16):
                plane = own[16 * pack + slot, :, tile * LANES : (tile + 1) * LANES]
                moved = pltpu.roll(plane, (8 * slot - begin) % LANES, 1)
                value = jnp.where(lane // 8 == slot, moved, value)
            s["far"][side, pack] = value
    each(place, counts, far, "start")
    field, far_land = s["field"], s["far_land"]
    if padded:
        field[8 : 8 + block[0], 0 : block[1], 0 : plan.width] = own[...]
    for dim, step in ((0, -1), (0, 1), (1, -1), (1, 1), (2, -1), (2, 1)):
        steps = tuple(step if which == dim else 0 for which in range(3))

        @pl.when(jnp.logical_not(exists(place, steps, counts)))
        def _():
            if dim == 0:
                begin = 0 if step < 0 else 8 + block[0]
                field[begin : begin + 8] = jnp.zeros((8,) + field.shape[1:], F32)
                pack = 0 if step < 0 else plan.far_packs + 1
                far_land[:, pack] = jnp.zeros((2,) + far_land.shape[2:], F32)
            if dim == 1:
                begin = block[1] if step > 0 else block[1] + 8
                field[:, begin : begin + 8] = jnp.zeros((field.shape[0], 8, field.shape[2]), F32)
                far_land[:, :, begin : begin + 8] = jnp.zeros(far_land.shape[:2] + (8, LANES), F32)
            if dim == 2:
                far_land[(1 - step) // 2] = jnp.zeros(far_land.shape[1:], F32)

    each(place, counts, part, "wait_recv", reverse=True)
    gather_part(plan, s)
    even_next = parity_of(next_.rows, LANES)
    n = next_.count
    next_.first(s, "next", 0, n)
    next_.half(s, "next", 1, even_next, 1, n - 1)
    next_.half(s, "next", 0, even_next, 2, n - 2)
    next_.half(s, "next", 1, even_next, 2, n - 2)
    pairs = s["pairs"]
    rows1 = plan.block1[1]
    height = max(rows1, 16)
    if rows1 < height:
        pairs[0 : next_.inner, rows1:height] = jnp.zeros((next_.inner, height - rows1, LANES), F32)
    for number, value in next_.residue(s, "next", even_next, 3, n - 3):
        pairs[number - 3, 0:rows1] = value[0:rows1]
    flat = pair_sums(pairs, height, next_.inner).reshape(next_.inner * (height // 2), LANES)
    row, column = iota((LANES, LANES), 0), iota((LANES, LANES), 1)
    down = weights((LANES, LANES), (row // 2 == column) & (row < plan.block1[2]), 0.5)
    below = dot(flat, down).reshape(next_.inner, height // 2, LANES)
    length = plan.block2
    per = LANES // length[2]
    packed = jnp.zeros((8, LANES), F32)
    for plane in range(length[0]):
        moved = below[plane]
        if plane // per:
            moved = pltpu.roll(moved, length[1] * (plane // per), 0)
        if plane % per:
            moved = pltpu.roll(moved, length[2] * (plane % per), 1)
        packed = packed + moved
    s["mine"][...] = packed
    slots = s["slots"]
    slots[me] = packed

    def send(number, slot):
        target, other = peer(number)
        return pltpu.make_async_remote_copy(
            src_ref=s["mine"],
            dst_ref=slots.at[me if slot is None else other],
            send_sem=s["sem_sent"].at[other],
            recv_sem=s["sem_got"].at[me if slot is None else other],
            device_id=target,
            device_id_type=MESH,
        )

    def start_send(number, carry):
        send(number, None).start()
        return carry

    lax.fori_loop(1, total, start_send, 0)
    swap = Exchange(next_, place, counts, s["nextB"], [s[f"swap{number}"] for number in range(8)])
    swap.start_xy()

    each(place, counts, far, "wait_recv", reverse=True)
    if not padded:
        loads[1].wait()
    base = wide.lanes - LANES
    shape = (wide.rows, LANES)
    lane = iota(shape, 1)
    even_wide = parity_of(wide.rows, wide.lanes)
    above = block[2] - base

    def wide_plane(number):
        pack, slot = (number + 8) // 16, (number + 8) % 16
        high = pltpu.roll(far_land[0, pack], (above - 8 * slot) % LANES, 1)
        low = pltpu.roll(far_land[1, pack], (LANES - 8 - 8 * slot) % LANES, 1)
        old = field[number, :, 0:LANES] if base == 0 else 0.0
        value = jnp.where((lane >= above) & (lane < above + 8), high, old)
        value = jnp.where(lane >= LANES - 8, low, value)
        return value if base == 0 else jnp.concatenate([field[number, :, 0:base], value], axis=1)

    for number in range(wide.count):
        one, two = wide_plane(2 * number), wide_plane(2 * number + 1)
        s["widef"][number] = jnp.where(even_wide, one, two)
        s["wideg"][number] = jnp.where(even_wide, two, one)
    n = wide.count
    wide.first(s, "wide", 0, n)
    wide.half(s, "wide", 1, even_wide, 1, n - 1)
    wide.half(s, "wide", 0, even_wide, 1, n - 1)
    wide.half(s, "wide", 1, even_wide, 2, n - 2)
    wider = iota((8, wide.lanes), 0) < 4

    def narrow(value):
        both = jnp.where(wider, value[block[1] : block[1] + 8], value[block[1] + 8 :])
        value = jnp.concatenate([value[: block[1]], both], axis=0)
        if top.lanes != wide.lanes:
            value = jnp.concatenate([value[:, : top.lanes - LANES], value[:, -LANES:]], axis=1)
        return value

    shift = wide.margins[0] - top.margins[0]
    for number in range(count):
        s["topf"][number] = narrow(s["widef"][number + shift])
        s["topg"][number] = narrow(s["wideg"][number + shift])
        s["topB"][number + 1] = narrow(s["wideB"][number + shift + 1])

    swap.finish_xy()
    swap.start_z()

    def finish_send(number, carry):
        copy = send(number, 0)
        copy.wait_recv()
        copy.wait_send()
        return carry

    lax.fori_loop(1, total, finish_send, 0)
    lane = iota((8, LANES), 1)
    whole = s["whole"]
    first = plan.levels[0]

    def place_x(which, carry):
        for second in range(counts[1]):
            start = (which * counts[1] + second) * counts[2]
            tiles = [slots[start + third] for third in range(counts[2])]
            for spot in range(per):
                value = jnp.zeros((8, LANES), F32)
                for third in range(counts[2]):
                    turn = (length[2] * (third - spot)) % LANES
                    moved = pltpu.roll(tiles[third], turn, 1) if turn else tiles[third]
                    value = jnp.where(lane // length[2] == third, moved, value)
                for group in range(8 // length[1]):
                    plane = which * length[0] + group * per + spot
                    whole[plane, second * length[1] : (second + 1) * length[1], :] = value[
                        group * length[1] : (group + 1) * length[1]
                    ]
        return carry

    lax.fori_loop(0, counts[0], place_x, 0)
    even_first = parity_of(first.rows, LANES)
    for number in range(first.count):
        one, two = whole[2 * number], whole[2 * number + 1]
        s["level0f"][number] = jnp.where(even_first, one, two)
        s["level0g"][number] = jnp.where(even_first, two, one)
    fill.wait()
    solve(plan, s, 0)
    solved = s["solved"]
    for number in range(3):
        solved[number] = jnp.zeros((first.rows, LANES), F32)
        solved[first.block[0] + 3 + number] = jnp.zeros((first.rows, LANES), F32)
    for plane in range(first.block[0]):
        solved[plane + 3] = first.planes(s, "level0", even_first, plane)

    swap.finish_z()
    shape = (LANES, LANES)
    index = iota(shape, 1)
    spot = local_of(index, plan.block1[2], 8, LANES)
    used = (index < plan.block1[2] + 8) | (index >= LANES - 8)
    lanes_to = weights(shape, (half_down(spot) + place[2] * length[2] == iota(shape, 0)) & used, 1.0)
    n = next_.count
    flat = jnp.concatenate([solved[place[0] * length[0] + number] for number in range(n)], axis=0)
    flat = dot(flat, lanes_to).reshape(n, first.rows, LANES)
    spread = s["spread"]
    spread[:, 0:16] = jnp.zeros((n, 16, LANES), F32)
    spread[:, 16 + 2 * first.rows :] = jnp.zeros((n, 16, LANES), F32)
    spread[0:n, pl.ds(16, first.rows, stride=2), :] = flat
    spread[0:n, pl.ds(17, first.rows, stride=2), :] = flat
    start = 16 + place[1] * rows1
    for number in range(n):
        tiles = [
            spread[number, pl.ds(pl.multiple_of(start + shift, 8), size), :]
            for shift, size in ((0, rows1), (rows1, 8), (-8, 8))
        ]
        s["nextB"][number + 1] = s["nextB"][number + 1] + jnp.concatenate(tiles, axis=0)
    for colour, skip in ((0, 0), (1, 1), (0, 1), (1, 2)):
        next_.half(s, "next", colour, even_next, skip, n - skip)

    pick = iota((8, LANES), 0) < 4
    planes = []
    for number in range(count):
        value = next_.planes(s, "next", even_next, number + 2 * next_.margins[0] - top.margins[0])
        edge = jnp.where(pick, value[rows1 : rows1 + 8], value[rows1 + 8 :])
        planes.append(jnp.concatenate([value[:rows1], edge], axis=0))
    shape = (LANES, top.lanes)
    cell, used = fine_cell(shape, 1)
    spreading = weights(shape, (cell == iota(shape, 0)) & used, 1.0)
    flat = dot(jnp.concatenate(planes, axis=0), spreading).reshape(count, plan.high, top.lanes)
    for tile in range(plan.tiles):
        piece = flat[:, :, tile * LANES : (tile + 1) * LANES]
        s[f"rows{tile}"][0:count, pl.ds(0, plan.high, stride=2), :] = piece
        s[f"rows{tile}"][0:count, pl.ds(1, plan.high, stride=2), :] = piece
    for number in range(count):
        tiles = []
        for tile in range(plan.tiles):
            rows = s[f"rows{tile}"]
            edge = jnp.where(pick, rows[number, block[1] : block[1] + 8], rows[number, block[1] + 8 : block[1] + 16])
            tiles.append(jnp.concatenate([rows[number, 0 : block[1]], edge], axis=0))
        s["topB"][number + 1] = s["topB"][number + 1] + jnp.concatenate(tiles, axis=1)
    top.half(s, "top", 0, even_top, 0, count)
    top.half(s, "top", 1, even_top, 1, count - 1)
    top.half(s, "top", 0, even_top, 1, count - 1)
    red = s["topR"]
    even_out = parity_of(block[1], block[2])
    for number, value in top.totals(red, even_top, 1, top.margins[0], count - top.margins[0]):
        black = ((s["topg"][number] + value) * inverse)[0 : block[1], 0 : block[2]]
        old = red[number + 1][0 : block[1], 0 : block[2]]
        plane = 2 * (number - top.margins[0])
        potential[plane] = jnp.where(even_out, old, black)
        potential[plane + 1] = jnp.where(even_out, black, old)
    each(place, counts, part, "wait_send")
    each(place, counts, far, "wait_send")
    swap.drain()


def cycle_matrix(size, depth):
    def beside_sum(v):
        p = np.pad(v, ((0, 0), (1, 1), (1, 1), (1, 1)))
        total = p[:, 2:, 1:-1, 1:-1] + p[:, :-2, 1:-1, 1:-1] + p[:, 1:-1, 2:, 1:-1] + p[:, 1:-1, :-2, 1:-1]
        return total + along * (p[:, 1:-1, 1:-1, 2:] + p[:, 1:-1, 1:-1, :-2])

    def cycle(g, left):
        parity = np.indices(g.shape[1:]).sum(0) % 2

        def sweeps(v, number):
            for _ in range(number):
                for colour in (0, 1):
                    v = np.where(parity == colour, (g + beside_sum(v)) / centre, v)
            return v

        v = np.zeros_like(g)
        if left == 0:
            return sweeps(v, CSWEEPS)
        v = sweeps(v, 2)
        r = g - centre * v + beside_sum(v)
        x, y, z = (part // 2 for part in g.shape[1:])
        coarse = 4 * r.reshape(-1, x, 2, y, 2, z, 2).mean((2, 4, 6))
        e = cycle(coarse, left - 1)
        for dim in (1, 2, 3):
            e = np.repeat(e, 2, dim)
        return sweeps(v + e, 2)

    cells = size[0] * size[1] * size[2]
    found = cycle(np.eye(cells).reshape((cells,) + size), depth).reshape(cells, cells)
    parts = []
    for _ in range(3):
        parts.append(found.astype(np.float32).astype(jnp.bfloat16))
        found = found - parts[-1].astype(np.float64)
    return np.stack(parts)


def on_device(counts, density):
    plan = Plan(density.shape, counts)
    scratch = plan.scratch()
    matrix = jnp.asarray(cycle_matrix(plan.dense, LEVELS - 1 - plan.dense_level))
    return pl.pallas_call(
        functools.partial(kernel, plan, list(scratch)),
        out_shape=jax.ShapeDtypeStruct(density.shape, F32),
        in_specs=[pl.BlockSpec(memory_space=pltpu.HBM)] * 2,
        out_specs=pl.BlockSpec(memory_space=pltpu.VMEM),
        scratch_shapes=list(scratch.values()),
        compiler_params=pltpu.CompilerParams(
            collective_id=0, has_side_effects=True, vmem_limit_bytes=48 * 1024 * 1024
        ),
    )(density, matrix)


def solution(mesh):
    counts = tuple(mesh.shape[axis] for axis in AXES)
    return jax.shard_map(
        functools.partial(on_device, counts),
        mesh=mesh,
        in_specs=(P("gx", "gy", "gz"),),
        out_specs=P("gx", "gy", "gz"),
        check_vma=False,
    )
```

time: 40.7 us -> 28.6 us (0.70)
  Pallas kernels: 38.8 us -> 25.4 us
  local copies, waits for them, and re-layouts: 1.65 us -> 3.06 us
    pallas_call x1, Pallas kernels: 38.8 us -> 25.4 us  [on_device(): pl.pallas_call(functools.partial(kernel, plan, list(scratch)), out_shape=...]
    unnamed x3 -> x5, local copies, waits for them, and re-layouts: 1.65 us -> 3.06 us
where the time goes in v1:
time: 28.6 us; the launch traced here: 28.4 us
  Pallas kernels  25.4 us (89%)
  local copies, waits for them, and re-layouts  3.06 us (11%)
    pallas_call x1, Pallas kernels, on_device(): pl.pallas_call(functools.partial(kernel, plan, list(scratch)), out_shape=...  25.4 us
    unnamed x5, local copies, waits for them, and re-layouts  3.06 us

profile of v1, /device:TPU:0, one launch (start us, length us, event | category | flops | bytes accessed | tf_op | source)
XLA Modules:
  0.0 28.4 jit_solution(11013597865494660579)
XLA Ops:
  0.0 0.0 copy-start
  0.0 1.4 %copy-done = bf16[3,512,512]{2,1,0:T(8,128)(2,1)S(1)} copy-done((bf16[3,512,512]{2,1,0:T(8,128)(2,1)S(1)}, bf16[3,512,512]{2,1,0:T(8,128)(2,1)}, u32[]{:S(2)}) %copy-start) | copy-done | bytes 1572888
  1.4 0.0 copy-start.1
  1.4 0.9 %copy-done.1 = f32[32,16,128]{2,1,0:T(8,128)S(1)} copy-done((f32[32,16,128]{2,1,0:T(8,128)S(1)}, f32[32,16,128]{2,1,0:T(8,128)}, u32[]{:S(2)}) %copy-start.1) | copy-done | bytes 262168
  2.4 25.4 %shard_map.28 = f32[32,16,128]{2,1,0:T(8,128)S(1)} custom-call(f32[32,16,128]{2,1,0:T(8,128)S(1)} %copy-done.1, bf16[3,512,512]{2,1,0:T(8,128)(2,1)S(1)} %copy-done), custom_call_target="tpu_custom_call" | custom-call | tf_op jit(solution)/shard_map/pallas_call | solution.py:1048
  27.7 0.7 %copy.4 = f32[32,16,128]{2,1,0:T(8,128)} copy(f32[32,16,128]{2,1,0:T(8,128)S(1)} %shard_map.28) | data formatting | bytes 524288
Async XLA Ops:
  0.0 1.4 %copy-start = (bf16[3,512,512]{2,1,0:T(8,128)(2,1)S(1)}, bf16[3,512,512]{2,1,0:T(8,128)(2,1)}, u32[]{:S(2)}) copy-start(bf16[3,512,512]{2,1,0:T(8,128)(2,1)} %constant.2.clone.dense) | copy-start | bytes 4718596
  1.4 0.9 %copy-start.1 = (f32[32,16,128]{2,1,0:T(8,128)S(1)}, f32[32,16,128]{2,1,0:T(8,128)}, u32[]{:S(2)}) copy-start(f32[32,16,128]{2,1,0:T(8,128)} %density.1) | copy-start | bytes 786436

commit v2 on v1

v2 whole, which is shorter than its diff:
```python
import functools
import types

import jax
import jax.numpy as jnp
import numpy as np
from jax import lax
from jax.experimental import pallas as pl
from jax.experimental.pallas import tpu as pltpu
from jax.sharding import PartitionSpec as P

LEVELS = 7
CSWEEPS = 4
DENSE = 512
rsd_beta = 0.5
centre = 4.0 + 2.0 * (1.0 + rsd_beta)
along = 1.0 + rsd_beta
inverse = 1.0 / centre
F32 = jnp.float32
BF16 = jnp.bfloat16
LANES = 128
AXES = ("gx", "gy", "gz")
MESH = pl.DeviceIdType.MESH
DIRECTIONS = [
    (dx, dy, dz) for dx in (-1, 0, 1) for dy in (-1, 0, 1) for dz in (-1, 0, 1) if (dx, dy, dz) != (0, 0, 0)
]


ALL, PART, FAR, SWAP, OWN, FIELD, MATRIX = 0, 2, 4, 6, 8, 9, 10


def up_to(value, unit):
    return -(-value // unit) * unit


def iota(shape, dim):
    return lax.broadcasted_iota(jnp.int32, shape, dim)


def pieces(value):
    high = value.astype(BF16)
    rest = value - high.astype(F32)
    middle = rest.astype(BF16)
    return high, middle, (rest - middle.astype(F32)).astype(BF16)


def product(left, right):
    return jnp.dot(left, right, preferred_element_type=F32)


def dot(value, chosen):
    chosen = chosen.astype(BF16)
    parts = [product(part, chosen) for part in pieces(value)]
    return parts[0] + (parts[1] + parts[2])


def local_of(index, length, margin, total):
    return jnp.where(index < total - margin, index, index - total)


def half_down(value):
    return jnp.where(value >= 0, lax.div(value, 2), -lax.div(1 - value, 2))


def parity_of(rows, lanes):
    return (iota((rows, lanes), 0) + iota((rows, lanes), 1)) % 2 == 0


def beside(below, here, above, even, colour, edge):
    rows, lanes = here.shape
    down, up = pltpu.roll(here, 1, 0), pltpu.roll(here, rows - 1, 0)
    left, right = pltpu.roll(here, 1, 1), pltpu.roll(here, lanes - 1, 1)
    if edge is not None:
        if edge[0] == rows:
            row = iota(here.shape, 0)
            down = jnp.where(row == 0, 0.0, down)
            up = jnp.where(row == rows - 1, 0.0, up)
        if edge[1] == lanes:
            lane = iota(here.shape, 1)
            left = jnp.where(lane == 0, 0.0, left)
            right = jnp.where(lane == lanes - 1, 0.0, right)
    other = jnp.where(even, below, above) if colour == 0 else jnp.where(even, above, below)
    return (here + other) + (down + up) + along * (left + right)


class Grid:
    def __init__(self, block, margins, edge=False):
        self.block, self.margins = block, margins
        self.inner = block[0] // 2
        self.count = self.inner + 2 * margins[0]
        self.rows = up_to(block[1] + 2 * margins[1], 8)
        self.lanes = up_to(block[2] + 2 * margins[2], LANES)
        self.edge = (block[1], block[2]) if edge else None

    def scratch(self):
        field = (self.count + 2, self.rows, self.lanes)
        source = (self.count, self.rows, self.lanes)
        return dict(
            R=pltpu.VMEM(field, F32),
            B=pltpu.VMEM(field, F32),
            f=pltpu.VMEM(source, F32),
            g=pltpu.VMEM(source, F32),
            m=pltpu.VMEM((3, self.rows, self.lanes), F32),
        )

    def zone(self, number):
        if number < self.margins[0]:
            return 0
        return 2 if number >= self.count - self.margins[0] else 1

    def guard(self, v):
        empty = jnp.zeros((self.rows, self.lanes), F32)
        for ref in (v.R, v.B):
            ref[0] = empty
            ref[self.count + 1] = empty

    def masks(self, v, place, counts):
        inside = None
        shape = (self.rows, self.lanes)
        for dim in (1, 2):
            index = iota(shape, dim - 1)
            size = shape[dim - 1]
            margin, length = self.margins[dim], self.block[dim]
            used = (index < length + margin) | (index >= size - margin)
            spot = local_of(index, length, margin, size) + place[dim] * length
            used = used & (spot >= 0) & (spot < length * counts[dim])
            inside = used if inside is None else inside & used
        value = jnp.where(inside, inverse, 0.0).astype(F32)
        v.m[1] = value
        if self.margins[0]:
            low = jnp.where(place[0] > 0, 1.0, 0.0).astype(F32)
            high = jnp.where(place[0] < counts[0] - 1, 1.0, 0.0).astype(F32)
            v.m[0] = value * low
            v.m[2] = value * high

    def first(self, v, begin, end):
        for number in range(begin, end):
            v.R[number + 1] = v.f[number] * v.m[self.zone(number)]

    def totals(self, other, even, colour, begin, end):
        before, here = other[begin], other[begin + 1]
        for number in range(begin, end):
            after = other[number + 2]
            yield number, beside(before, here, after, even, colour, self.edge)
            before, here = here, after

    def half(self, v, colour, even, begin, end):
        target, other = (v.R, v.B) if colour == 0 else (v.B, v.R)
        source = v.f if colour == 0 else v.g
        for number, total in self.totals(other, even, colour, begin, end):
            target[number + 1] = (source[number] + total) * v.m[self.zone(number)]

    def residue(self, v, even, begin, end):
        for number, total in self.totals(v.B, even, 0, begin, end):
            yield number, v.f[number] - centre * v.R[number + 1] + total

    def planes(self, v, even, plane):
        red, black = v.R[plane // 2 + 1], v.B[plane // 2 + 1]
        return jnp.where(even, red, black) if plane % 2 == 0 else jnp.where(even, black, red)


def exists(place, steps, counts):
    found = None
    for which in range(3):
        if steps[which] == 0:
            continue
        other = place[which] + steps[which]
        here = (other >= 0) & (other < counts[which])
        found = here if found is None else found & here
    return found


def device(place, steps):
    return tuple(place[which] + steps[which] for which in range(3))


class Plan:
    def __init__(self, block, counts):
        self.counts, self.block = counts, block
        self.total = counts[0] * counts[1] * counts[2]
        self.block1 = tuple(size // 2 for size in block)
        self.block2 = tuple(size // 4 for size in block)
        self.top = Grid(block, (2, 4, 4))
        self.wide = Grid(block, (4, 8, 8))
        self.next = Grid(self.block1, (3, 8, 8))
        self.width = up_to(block[2], LANES)
        self.tiles = self.top.lanes // LANES
        self.count = self.top.count
        self.high = self.block1[1] + 8
        self.per = LANES // self.block1[2]
        self.side = 8 // self.per
        self.middle = (self.count - 16) // self.per
        self.vectors = 2 * self.side + self.middle + 1
        self.packs = 1 + (self.count > 16)
        self.far_packs = block[0] // 16
        assert block[0] % 16 == 0 and self.block1[1] % 8 == 0 and self.block2[2] <= LANES
        assert self.next.lanes == LANES and (self.count - 16) % self.per == 0 and 64 % self.block1[2] == 0
        self.levels = []
        size = tuple(block[which] * counts[which] // 4 for which in range(3))
        number = 2
        while size[0] * size[1] * size[2] > DENSE:
            self.levels.append(Grid(size, (0, 0, 0), edge=True))
            assert self.levels[-1].lanes == LANES
            size = tuple(part // 2 for part in size)
            number += 1
        self.dense, self.dense_level = size, number

    def message(self, steps):
        dx, dy, dz = steps
        if dz == 0:
            begin, length = {0: (0, self.vectors), -1: (0, self.side + 1), 1: (self.side, self.side + 1)}[dx]
            if dy == 0:
                return ("part_t", (pl.ds(begin, length),), (length, self.high, LANES))
            return ("part_y", ((dy + 1) // 2, pl.ds(begin, length)), (length, 8, LANES))
        length = self.packs if dx == 0 else 1
        if dy == 0:
            return ("part_z", ((dz + 1) // 2, pl.ds(0, length)), (length, self.high, LANES))
        return (
            "part_zy", ((dz + 1) // 2, (dy + 1) // 2, pl.ds(0, length)), (length, 8, LANES),
        )

    def scratch(self):
        block = self.block
        s = types.SimpleNamespace(
            top=self.top.scratch(), wide=self.wide.scratch(), next=self.next.scratch(),
            levels=[grid.scratch() for grid in self.levels],
        )
        s.own = pltpu.VMEM((block[0], block[1], self.width), F32)
        if block[2] != self.width:
            s.raw = pltpu.VMEM(block, F32)
        s.field = pltpu.VMEM((block[0] + 16, block[1] + 16, self.wide.lanes), F32)
        s.rows = [pltpu.VMEM((self.count, block[1] + 16, LANES), F32) for _ in range(self.tiles)]
        s.part = pltpu.VMEM((self.count, self.high, LANES), F32)
        s.part_t = pltpu.VMEM((self.vectors, self.high, LANES), F32)
        s.part_y = pltpu.VMEM((2, self.vectors, 8, LANES), F32)
        s.part_z = pltpu.VMEM((2, self.packs, self.high, LANES), F32)
        s.part_zy = pltpu.VMEM((2, 2, self.packs, 8, LANES), F32)
        s.land = [pltpu.VMEM(self.message(steps)[2], F32) for steps in DIRECTIONS]
        s.sums, s.sumz = [], []
        wide_rows = self.block1[1] + 16
        for dx in (-1, 0, 1):
            length = self.vectors if dx == 0 else self.side + 1
            packs = self.packs if dx == 0 else 1
            s.sums.append(pltpu.VMEM((length, wide_rows, LANES), F32))
            s.sumz.append(pltpu.VMEM((2, packs, wide_rows, LANES), F32))
        s.far = pltpu.VMEM((2, self.far_packs, block[1], LANES), F32)
        s.far_land = pltpu.VMEM((2, self.far_packs + 2, block[1] + 16, LANES), F32)
        s.swap = pltpu.VMEM((2, self.block1[1], LANES), F32)
        s.swap_land = pltpu.VMEM((self.next.count, self.next.rows, LANES), F32)
        s.swap_side = pltpu.VMEM((2, 3, self.next.rows, LANES), F32)
        first = self.levels[0]
        coarse = [first] + self.levels[1:]
        s.pairs = pltpu.VMEM((max(g.block[0] for g in coarse + [self.next]), 2 * up_to(first.rows, 16), LANES), F32)
        s.solved = pltpu.VMEM((first.block[0] + 6, first.rows, LANES), F32)
        s.spread = pltpu.VMEM((self.next.count, 2 * first.rows + 32, LANES), F32)
        s.whole = pltpu.VMEM((first.block[0], first.rows, LANES), F32)
        s.mine = pltpu.VMEM((8, LANES), F32)
        s.slots = pltpu.VMEM((self.total, 8, LANES), F32)
        size = self.dense[0] * self.dense[1] * self.dense[2]
        s.matrix = pltpu.VMEM((3, size, size), BF16)
        most = max(sum(size(self, steps) for steps in DIRECTIONS) for size in (size_part, size_far, size_swap))
        s.bytes = pltpu.VMEM((max(most, self.total), 8, LANES), F32)
        s.sem = pltpu.SemaphoreType.DMA((MATRIX + 1,))
        return vars(s)


def weights(shape, found, value):
    return jnp.where(found, value, 0.0).astype(F32).reshape(shape)


def pair_sums(s, height, count):
    even = s[0:count, pl.ds(0, height // 2, stride=2), :]
    return even + s[0:count, pl.ds(1, height // 2, stride=2), :]


def named(value):
    if isinstance(value, dict):
        return types.SimpleNamespace(**value)
    return [named(one) for one in value] if isinstance(value, list) else value


def sem(s, number):
    return s.sem.at[number]


def size_part(plan, steps):
    shape = plan.message(steps)[2]
    return shape[0] * shape[1] // 8


def size_far(plan, steps):
    rows = plan.block[1] // 8 if steps[1] == 0 else 1
    if steps[2]:
        return rows * (plan.far_packs if steps[0] == 0 else 1)
    return rows * (plan.block[0] if steps[0] == 0 else 8) * (plan.width // LANES)


def size_swap(plan, steps):
    rows = plan.block1[1] // 8 if steps[1] == 0 else 1
    return rows if steps[2] else rows * (plan.next.inner if steps[0] == 0 else plan.next.margins[0])


def wait_all(plan, s, place, size, name, other):
    counts = plan.counts
    beside_of = [
        jnp.where(place[axis] > 0, 1, 0) + jnp.where(place[axis] < counts[axis] - 1, 1, 0) for axis in range(3)
    ]
    choices = [{1: (0,), 2: (1,)}.get(count, (1, 2)) for count in counts]
    for x in choices[0]:
        for y in choices[1]:
            for z in choices[2]:
                number = 0
                for steps in DIRECTIONS:
                    many = [1 if step == 0 else (have if step > 0 else 0) for step, have in zip(steps, (x, y, z))]
                    if min(steps) >= 0:
                        number += many[0] * many[1] * many[2] * size(plan, steps)
                if number == 0:
                    continue
                found = (beside_of[0] == x) & (beside_of[1] == y) & (beside_of[2] == z)

                @pl.when(found)
                def _():
                    pltpu.make_async_remote_copy(
                        src_ref=s.bytes.at[pl.ds(0, number)],
                        dst_ref=s.bytes.at[pl.ds(0, number)],
                        send_sem=sem(s, name),
                        recv_sem=sem(s, name),
                        device_id=other,
                        device_id_type=MESH,
                    ).wait_recv()


def send_part(plan, s, place, number):
    steps = DIRECTIONS[number]
    name, index, _ = plan.message(steps)
    return pltpu.make_async_remote_copy(
        src_ref=getattr(s, name).at[index],
        dst_ref=s.land[number],
        send_sem=sem(s, PART),
        recv_sem=sem(s, PART + 1),
        device_id=device(place, steps),
        device_id_type=MESH,
    )


def send_far(plan, s, place, number):
    dx, dy, dz = steps = DIRECTIONS[number]
    block = plan.block
    rows = {0: (0, block[1], 0), 1: (block[1] - 8, 8, block[1] + 8), -1: (0, 8, block[1])}[dy]
    if dz == 0:
        planes = {0: (0, block[0], 8), 1: (block[0] - 8, 8, 0), -1: (0, 8, block[0] + 8)}[dx]
        source = s.own.at[pl.ds(planes[0], planes[1]), pl.ds(rows[0], rows[1]), :]
        target = s.field.at[pl.ds(planes[2], planes[1]), pl.ds(rows[2], rows[1]), pl.ds(0, plan.width)]
    else:
        side, last = (dz + 1) // 2, plan.far_packs - 1
        packs = {0: (0, last + 1, 1), 1: (last, 1, 0), -1: (0, 1, last + 2)}[dx]
        source = s.far.at[side, pl.ds(packs[0], packs[1]), pl.ds(rows[0], rows[1]), :]
        target = s.far_land.at[side, pl.ds(packs[2], packs[1]), pl.ds(rows[2], rows[1]), :]
    return pltpu.make_async_remote_copy(
        src_ref=source,
        dst_ref=target,
        send_sem=sem(s, FAR),
        recv_sem=sem(s, FAR + 1),
        device_id=device(place, steps),
        device_id_type=MESH,
    )


def send_swap(plan, s, place, number):
    dx, dy, dz = steps = DIRECTIONS[number]
    high, margin, inner = plan.block1[1], plan.next.margins[0], plan.next.inner
    rows = {0: (0, high, 0), 1: (high - 8, 8, high + 8), -1: (0, 8, high)}[dy]
    if dz == 0:
        planes = {0: (margin, inner, margin), 1: (inner, margin, 0), -1: (margin, margin, margin + inner)}[dx]
        source = s.next.B.at[pl.ds(1 + planes[0], planes[1]), pl.ds(rows[0], rows[1]), :]
        target = s.swap_land.at[pl.ds(planes[2], planes[1]), pl.ds(rows[2], rows[1]), :]
    else:
        side = (dz + 1) // 2
        source = s.swap.at[side, pl.ds(rows[0], rows[1]), :]
        target = s.swap_side.at[side, 1 - dx, pl.ds(rows[2], rows[1]), :]
    return pltpu.make_async_remote_copy(
        src_ref=source,
        dst_ref=target,
        send_sem=sem(s, SWAP),
        recv_sem=sem(s, SWAP + 1),
        device_id=device(place, steps),
        device_id_type=MESH,
    )


def pack_swap(plan, s):
    length, margin = plan.block1[2], plan.next.margins[0]
    lane = iota((plan.block1[1], LANES), 1)
    for side in range(2):
        begin = 0 if side == 0 else length - 8
        value = jnp.zeros(lane.shape, F32)
        for slot in range(plan.next.inner):
            plane = s.next.B[1 + margin + slot, 0 : plan.block1[1], :]
            value = jnp.where(lane // 8 == slot, pltpu.roll(plane, (8 * slot - begin) % LANES, 1), value)
        s.swap[side] = value


def swapped(plan, s, number):
    length, rows = plan.block1[2], plan.block1[1]
    margin, inner = plan.next.margins[0], plan.next.inner
    lane = iota((plan.next.rows, LANES), 1)
    which = 0 if number < margin else (2 if number >= margin + inner else 1)
    slot = number - margin + (1 - which) * inner
    value = s.swap_land[number]
    if which == 1:
        value = jnp.concatenate([s.next.B[number + 1, 0:rows, :], value[rows:]], axis=0)
    high = pltpu.roll(s.swap_side[0, which], (length - 8 * slot) % LANES, 1)
    low = pltpu.roll(s.swap_side[1, which], (LANES - 8 - 8 * slot) % LANES, 1)
    edge = jnp.where(lane < length + 8, high, jnp.where(lane >= LANES - 8, low, 0.0))
    return jnp.where(lane < length, value, edge)


def partners(place, count):
    if count & (count - 1):
        return [(lax.rem(place + off, count), lax.rem(place + count - off, count)) for off in range(count)]
    bits = [lax.rem(lax.div(place, 1 << bit), 2) for bit in range(count.bit_length() - 1)]
    out = []
    for off in range(count):
        value = jnp.int32(0)
        for bit, digit in enumerate(bits):
            value = value + ((1 - digit) if off >> bit & 1 else digit) * (1 << bit)
        out.append((value, value))
    return out


def each(place, counts, send):
    for number, steps in enumerate(DIRECTIONS):
        @pl.when(exists(place, steps, counts))
        def _():
            send(number).start()


def pack_part(plan, s):
    count, per, side, middle, rows = plan.count, plan.per, plan.side, plan.middle, plan.block1[1]
    length = plan.block1[2]
    part = s.part
    shape = (plan.high, LANES)
    lane = iota(shape, 1)
    sub = iota((8, LANES), 0)

    def pair_y(value):
        edge = value[rows:]
        minus = jnp.where(sub >= 6, edge, value[:8])
        return minus, jnp.where(sub < 2, edge, value[rows - 8 : rows])

    groups = [(0, 0, side), (side + 1, count - 8, side), (2 * side + 1, 8, middle)]
    for index, first, number in groups:
        for spot in range(number):
            value = part[first + spot]
            for which in range(1, per):
                moved = pltpu.roll(part[first + spot + which * number], which * length, 1)
                value = jnp.where(lane // length == which, moved, value)
            s.part_t[index + spot] = value
            minus, plus = pair_y(value)
            s.part_y[0, index + spot] = minus
            s.part_y[1, index + spot] = plus
    value = jnp.zeros(shape, F32)
    couple = lane // 2
    for number in range(count):
        low = pltpu.roll(part[number], 2 * number, 1)
        high = low if length == 64 else pltpu.roll(part[number], 64 - length + 2 * number, 1)
        value = jnp.where(couple == ((126 + 2 * number) % LANES) // 2, low, value)
        value = jnp.where(couple == 32 + number, high, value)
    s.part_t[side] = value
    minus, plus = pair_y(value)
    s.part_y[0, side] = minus
    s.part_y[1, side] = plus
    for which in range(2):
        begin = LANES - 2 if which == 0 else length - 6
        for pack in range(plan.packs):
            value = jnp.zeros(shape, F32)
            planes = list(range(8)) + list(range(count - 8, count)) if pack == 0 else list(range(8, count - 8))
            for slot, number in enumerate(planes):
                moved = pltpu.roll(part[number], (8 * slot - begin) % LANES, 1)
                value = jnp.where(lane // 8 == slot, moved, value)
            s.part_z[which, pack] = value
            minus, plus = pair_y(value)
            s.part_zy[which, 0, pack] = minus
            s.part_zy[which, 1, pack] = plus


def gather_part(plan, s):
    side, count, rows, per, length = plan.side, plan.count, plan.block1[1], plan.per, plan.block1[2]
    sub = iota((8, LANES), 0)
    land = {steps: s.land[number] for number, steps in enumerate(DIRECTIONS)}

    def assembled(own, plus, minus):
        edge = own[rows:]
        tiles = [own[8 * number : 8 * number + 8] for number in range(rows // 8)]
        tiles[0] = tiles[0] + jnp.where(sub < 2, minus, 0.0)
        tiles[-1] = tiles[-1] + jnp.where(sub >= 6, plus, 0.0)
        tiles.append(jnp.where(sub < 6, plus, 0.0) + jnp.where(sub < 2, edge, 0.0))
        tiles.append(jnp.where(sub >= 2, minus, 0.0) + jnp.where(sub >= 6, edge, 0.0))
        return jnp.concatenate(tiles, axis=0)

    for dx in (-1, 0, 1):
        own = s.part_t if dx == 0 else land[(dx, 0, 0)]
        for index in range(own.shape[0]):
            s.sums[dx + 1][index] = assembled(own[index], land[(dx, -1, 0)][index], land[(dx, 1, 0)][index])
        for which in range(2):
            dz = 2 * which - 1
            for pack in range(land[(dx, 0, dz)].shape[0]):
                s.sumz[dx + 1][which, pack] = assembled(
                    land[(dx, 0, dz)][pack], land[(dx, -1, dz)][pack], land[(dx, 1, dz)][pack]
                )

    shape = (rows + 16, LANES)
    lane = iota(shape, 1)
    at_low, at_high = lane >= LANES - 2, (lane == length) | (lane == length + 1)
    inner = lane < length
    above = (lane >= length - 2) & (lane < length + 6)
    below = (lane >= LANES - 6) | (lane < 2)
    even = parity_of(*shape)

    def turned(value, shift):
        shift = shift % LANES
        return pltpu.roll(value, shift, 1) if shift else value

    def plane_of(dx, number):
        if number < 8:
            index, slots, size, first = number, number, side, 0
            base = 0
        elif number >= count - 8:
            index, slots, size, first = number - (count - 8), 8 + number - (count - 8), side, count - 8
            base = side + 1
        else:
            index, slots, size, first = number - 8, number - 8, plan.middle, 8
            base = 2 * side + 1
        pack = 0 if number < 8 or number >= count - 8 else 1
        extra = side
        if dx == -1:
            base, extra = 0, side
        if dx == 1:
            base, extra = 1, 0
        total = s.sums[dx + 1]
        main = turned(total[base + index % size], -(index // size) * length)
        low = turned(total[extra], -2 * number)
        high = low if length == 64 else turned(total[extra], length - 64 - 2 * number)
        value = jnp.where(inner, main, jnp.where(at_low, low, jnp.where(at_high, high, 0.0)))
        far = s.sumz[dx + 1]
        from_above = turned(far[0, pack], length - 2 - 8 * slots)
        from_below = turned(far[1, pack], LANES - 6 - 8 * slots)
        return value + (jnp.where(above, from_above, 0.0) + jnp.where(below, from_below, 0.0))

    def plane(number):
        spot = number - 2 * plan.next.margins[0]
        total = None
        for dx, place in ((0, spot), (-1, spot - plan.block1[0]), (1, spot + plan.block1[0])):
            index = place + 2
            allowed = {0: (0, count), -1: (0, 8), 1: (count - 8, count)}[dx]
            if allowed[0] <= index < allowed[1]:
                value = plane_of(dx, index)
                total = value if total is None else total + value
        return total

    for number in range(plan.next.count):
        first, second = plane(2 * number), plane(2 * number + 1)
        s.next.f[number] = jnp.where(even, first, second)
        s.next.g[number] = jnp.where(even, second, first)


def solve(plan, s, number):
    grid, v = plan.levels[number], s.levels[number]
    even = parity_of(grid.rows, LANES)
    count = grid.count
    grid.first(v, 0, count)
    for colour in (1, 0, 1):
        grid.half(v, colour, even, 0, count)
    pairs = s.pairs
    height = max(grid.rows, 16)
    if grid.rows < height:
        pairs[0:count, grid.rows : height] = jnp.zeros((count, height - grid.rows, LANES), F32)
    for spot, value in grid.residue(v, even, 0, count):
        if grid.rows > grid.block[1]:
            value = jnp.where(iota(value.shape, 0) < grid.block[1], value, 0.0)
        pairs[spot, 0 : grid.rows] = value
    flat = pair_sums(pairs, height, count).reshape(count * (height // 2), LANES)
    row, column = iota((LANES, LANES), 0), iota((LANES, LANES), 1)
    if number + 1 < len(plan.levels):
        below, under = plan.levels[number + 1], s.levels[number + 1]
        down = weights((LANES, LANES), (row // 2 == column) & (row < grid.block[2]), 0.5)
        coarse = dot(flat, down).reshape(count, height // 2, LANES)[:, : below.rows]
        same = parity_of(below.rows, LANES)
        for spot in range(below.count):
            one, two = coarse[2 * spot], coarse[2 * spot + 1]
            under.f[spot] = jnp.where(same, one, two)
            under.g[spot] = jnp.where(same, two, one)
        solve(plan, s, number + 1)
        planes = [below.planes(under, same, plane) for plane in range(count)]
        spread = weights((LANES, LANES), column // 2 == row, 1.0)
        flat = dot(jnp.concatenate(planes, axis=0), spread).reshape(count, below.rows, LANES)
        pairs[0:count, pl.ds(0, below.rows, stride=2), :] = flat
        pairs[0:count, pl.ds(1, below.rows, stride=2), :] = flat
        for spot in range(count):
            v.B[spot + 1] = v.B[spot + 1] + pairs[spot, 0 : grid.rows]
    else:
        nx, ny, nz = plan.dense
        size = nx * ny * nz
        tall = height // 2
        down = weights((LANES, LANES), (row // 2 == column % nz) & (row < grid.block[2]), 0.5)
        many = dot(flat, down).reshape(count, tall, LANES)
        wide = up_to(size, LANES) // LANES
        here, lane = iota((tall, LANES), 0), iota((tall, LANES), 1)
        parts = []
        for vector in range(wide):
            cell = (vector * LANES + lane) // nz
            total = jnp.zeros((tall, LANES), F32)
            for spot in range(nx):
                total = total + jnp.where((cell == spot * ny + here) & (here < ny), many[spot], 0.0)
            parts.append(total)
        left = jnp.concatenate(parts, axis=1)[:, :size]
        high, middle, low = pieces(left)
        stack = jnp.concatenate([high, middle, low], axis=0)
        matrix = s.matrix
        one = product(stack, matrix[0])
        two = product(stack[: 2 * tall], matrix[1])
        three = product(high, matrix[2])
        total = one[:tall] + ((one[tall : 2 * tall] + one[2 * tall :]) + ((two[:tall] + two[tall:]) + three))
        answer = jnp.sum(total, axis=0, keepdims=True)
        here, lane = iota((grid.rows, LANES), 0), iota((grid.rows, LANES), 1)
        planes = []
        for spot in range(nx):
            value = jnp.zeros((grid.rows, LANES), F32)
            for vector in range(wide):
                if (vector + 1) * LANES <= spot * ny * nz or vector * LANES >= (spot + 1) * ny * nz:
                    continue
                piece = jnp.broadcast_to(answer[:, vector * LANES : (vector + 1) * LANES], value.shape)
                cell = (vector * LANES + lane) // nz
                value = jnp.where(cell == spot * ny + here // 2, piece, value)
            planes.append(value)
        spread = weights((LANES, LANES), (column // 2 == row % nz) & (column < grid.block[2]), 1.0)
        flat = dot(jnp.concatenate(planes, axis=0), spread).reshape(count, grid.rows, LANES)
        for spot in range(count):
            v.B[spot + 1] = v.B[spot + 1] + flat[spot]
    for colour in (0, 1, 0, 1):
        grid.half(v, colour, even, 0, count)


def kernel(plan, tree, density, dense, potential, *refs):
    held = jax.tree.unflatten(tree, refs)
    s = types.SimpleNamespace(**{key: named(value) for key, value in held.items()})
    counts, block, total = plan.counts, plan.block, plan.total
    top, wide, next_ = plan.top, plan.wide, plan.next
    place = tuple(lax.axis_index(axis) for axis in AXES)
    me = (place[0] * counts[1] + place[1]) * counts[2] + place[2]
    padded = block[2] != plan.width

    loads = [pltpu.make_async_copy(density, s.raw if padded else s.own, sem(s, OWN))]
    loads[0].start()
    if not padded:
        loads.append(
            pltpu.make_async_copy(
                density,
                s.field.at[pl.ds(8, block[0]), pl.ds(0, block[1]), pl.ds(0, block[2])],
                sem(s, FIELD),
            )
        )
    fill = pltpu.make_async_copy(dense, s.matrix, sem(s, MATRIX))

    for ref in s.land + [s.swap_land, s.swap_side]:
        ref[...] = jnp.zeros(ref.shape, F32)

    axes = [partners(place[axis], counts[axis]) for axis in range(3)]
    offsets = [
        (a, b, c) for a in range(counts[0]) for b in range(counts[1]) for c in range(counts[2]) if (a, b, c) != (0, 0, 0)
    ]
    offsets.sort(key=lambda off: -(off[0] + off[1] + off[2] / 2))

    def peer(off, way):
        target = tuple(axes[axis][off[axis]][way] for axis in range(3))
        return target, (target[0] * counts[1] + target[1]) * counts[2] + target[2]

    other = peer(offsets[0], 0)[0]
    barrier = pltpu.get_barrier_semaphore()
    for off in offsets:
        pl.semaphore_signal(barrier, inc=1, device_id=peer(off, 0)[0], device_id_type=MESH)

    for ref in (s.top.f, s.top.g, s.top.R, s.top.B):
        ref[...] = jnp.zeros(ref.shape, F32)
    for v, grid in ((s.top, top), (s.wide, wide), (s.next, next_)):
        grid.guard(v)
        grid.masks(v, place, counts)
    for v, grid in zip(s.levels, plan.levels):
        grid.guard(v)
        grid.masks(v, (0, 0, 0), (1, 1, 1))
    loads[0].wait()
    for load in loads[1:] + [fill]:
        load.start()
    own = s.own
    if padded:
        own[...] = jnp.zeros(own.shape, F32)
        own[:, :, 0 : block[2]] = s.raw[...]

    even_own = parity_of(block[1], plan.width)
    for number in range(top.inner):
        one, two = own[2 * number], own[2 * number + 1]
        red = jnp.where(even_own, one, two)
        spot = number + top.margins[0]
        s.top.f[spot, 0 : block[1], 0 : plan.width] = red
        s.top.g[spot, 0 : block[1], 0 : plan.width] = jnp.where(even_own, two, one)
        s.top.R[spot + 1, 0 : block[1], 0 : plan.width] = red * inverse
    even_top = parity_of(top.rows, top.lanes)
    count = top.count
    top.half(s.top, 1, even_top, 1, count - 1)
    top.half(s.top, 0, even_top, 1, count - 1)
    top.half(s.top, 1, even_top, 0, count)
    for number, value in top.residue(s.top, even_top, 0, count):
        for tile in range(plan.tiles):
            piece = value[:, tile * LANES : (tile + 1) * LANES]
            s.rows[tile][number, 0 : top.rows] = piece
            s.rows[tile][number, top.rows : top.rows + 8] = piece[block[1] :]
    flat = jnp.concatenate(
        [
            pair_sums(s.rows[tile], block[1] + 16, count).reshape(count * plan.high, LANES)
            for tile in range(plan.tiles)
        ],
        axis=1,
    )

    def fine_cell(shape, dim):
        index = iota(shape, dim)
        used = (index < block[2] + 4) | (index >= top.lanes - 4)
        cell = half_down(local_of(index, block[2], 4, top.lanes))
        return jnp.where(cell < 0, cell + LANES, cell), used

    shape = (top.lanes, LANES)
    cell, used = fine_cell(shape, 0)
    down = weights(shape, (cell == iota(shape, 1)) & used, 0.5)
    s.part[...] = dot(flat, down).reshape(count, plan.high, LANES)
    pack_part(plan, s)

    pl.semaphore_wait(barrier, total - 1)
    part = functools.partial(send_part, plan, s, place)
    far = functools.partial(send_far, plan, s, place)
    each(place, counts, part)

    lane = iota((block[1], LANES), 1)
    for side in range(2):
        begin = 0 if side == 0 else block[2] - 8
        tile = begin // LANES
        for pack in range(plan.far_packs):
            value = jnp.zeros((block[1], LANES), F32)
            for slot in range(16):
                plane = own[16 * pack + slot, :, tile * LANES : (tile + 1) * LANES]
                moved = pltpu.roll(plane, (8 * slot - begin) % LANES, 1)
                value = jnp.where(lane // 8 == slot, moved, value)
            s.far[side, pack] = value
    each(place, counts, far)
    field, far_land = s.field, s.far_land
    if padded:
        field[8 : 8 + block[0], 0 : block[1], 0 : plan.width] = own[...]
    for dim, step in ((0, -1), (0, 1), (1, -1), (1, 1), (2, -1), (2, 1)):
        steps = tuple(step if which == dim else 0 for which in range(3))

        @pl.when(jnp.logical_not(exists(place, steps, counts)))
        def _():
            if dim == 0:
                begin = 0 if step < 0 else 8 + block[0]
                field[begin : begin + 8] = jnp.zeros((8,) + field.shape[1:], F32)
                pack = 0 if step < 0 else plan.far_packs + 1
                far_land[:, pack] = jnp.zeros((2,) + far_land.shape[2:], F32)
            if dim == 1:
                begin = block[1] if step > 0 else block[1] + 8
                field[:, begin : begin + 8] = jnp.zeros((field.shape[0], 8, field.shape[2]), F32)
                far_land[:, :, begin : begin + 8] = jnp.zeros(far_land.shape[:2] + (8, LANES), F32)
            if dim == 2:
                far_land[(1 - step) // 2] = jnp.zeros(far_land.shape[1:], F32)

    wait_all(plan, s, place, size_part, PART + 1, other)
    gather_part(plan, s)
    even_next = parity_of(next_.rows, LANES)
    n = next_.count
    next_.first(s.next, 0, n)
    next_.half(s.next, 1, even_next, 1, n - 1)
    next_.half(s.next, 0, even_next, 2, n - 2)
    next_.half(s.next, 1, even_next, 2, n - 2)
    pairs = s.pairs
    rows1 = plan.block1[1]
    height = max(rows1, 16)
    if rows1 < height:
        pairs[0 : next_.inner, rows1:height] = jnp.zeros((next_.inner, height - rows1, LANES), F32)
    for number, value in next_.residue(s.next, even_next, 3, n - 3):
        pairs[number - 3, 0:rows1] = value[0:rows1]
    flat = pair_sums(pairs, height, next_.inner).reshape(next_.inner * (height // 2), LANES)
    row, column = iota((LANES, LANES), 0), iota((LANES, LANES), 1)
    down = weights((LANES, LANES), (row // 2 == column) & (row < plan.block1[2]), 0.5)
    below = dot(flat, down).reshape(next_.inner, height // 2, LANES)
    length = plan.block2
    per = LANES // length[2]
    packed = jnp.zeros((8, LANES), F32)
    for plane in range(length[0]):
        moved = below[plane]
        if plane // per:
            moved = pltpu.roll(moved, length[1] * (plane // per), 0)
        if plane % per:
            moved = pltpu.roll(moved, length[2] * (plane % per), 1)
        packed = packed + moved
    s.mine[...] = packed
    slots = s.slots
    slots[me] = packed

    def send(number, slot):
        return pltpu.make_async_remote_copy(
            src_ref=s.mine,
            dst_ref=slots.at[slot],
            send_sem=sem(s, ALL),
            recv_sem=sem(s, ALL + 1),
            device_id=peer(offsets[number], 0)[0],
            device_id_type=MESH,
        )

    def start_sends():
        for number in range(total - 1):
            send(number, me).start()

    start_sends()
    swap = functools.partial(send_swap, plan, s, place)
    pack_swap(plan, s)
    each(place, counts, swap)

    wait_all(plan, s, place, size_far, FAR + 1, other)
    if not padded:
        loads[1].wait()
    base = wide.lanes - LANES
    shape = (wide.rows, LANES)
    lane = iota(shape, 1)
    even_wide = parity_of(wide.rows, wide.lanes)
    above = block[2] - base

    def wide_plane(number):
        pack, slot = (number + 8) // 16, (number + 8) % 16
        high = pltpu.roll(far_land[0, pack], (above - 8 * slot) % LANES, 1)
        low = pltpu.roll(far_land[1, pack], (LANES - 8 - 8 * slot) % LANES, 1)
        old = field[number, :, 0:LANES] if base == 0 else 0.0
        value = jnp.where((lane >= above) & (lane < above + 8), high, old)
        value = jnp.where(lane >= LANES - 8, low, value)
        return value if base == 0 else jnp.concatenate([field[number, :, 0:base], value], axis=1)

    for number in range(wide.count):
        one, two = wide_plane(2 * number), wide_plane(2 * number + 1)
        s.wide.f[number] = jnp.where(even_wide, one, two)
        s.wide.g[number] = jnp.where(even_wide, two, one)
    n = wide.count
    wide.first(s.wide, 0, n)
    wide.half(s.wide, 1, even_wide, 1, n - 1)
    wide.half(s.wide, 0, even_wide, 1, n - 1)
    wide.half(s.wide, 1, even_wide, 2, n - 2)
    wider = iota((8, wide.lanes), 0) < 4

    def narrow(value):
        both = jnp.where(wider, value[block[1] : block[1] + 8], value[block[1] + 8 :])
        value = jnp.concatenate([value[: block[1]], both], axis=0)
        if top.lanes != wide.lanes:
            value = jnp.concatenate([value[:, : top.lanes - LANES], value[:, -LANES:]], axis=1)
        return value

    shift = wide.margins[0] - top.margins[0]
    for number in range(count):
        s.top.f[number] = narrow(s.wide.f[number + shift])
        s.top.g[number] = narrow(s.wide.g[number + shift])
        s.top.B[number + 1] = narrow(s.wide.B[number + shift + 1])

    def finish_sends():
        for name in (ALL + 1, ALL):
            pltpu.make_async_remote_copy(
                src_ref=s.bytes.at[pl.ds(0, total - 1)],
                dst_ref=s.bytes.at[pl.ds(0, total - 1)],
                send_sem=sem(s, name),
                recv_sem=sem(s, name),
                device_id=other,
                device_id_type=MESH,
            ).wait_recv()

    finish_sends()
    lane = iota((8, LANES), 1)
    whole = s.whole
    first = plan.levels[0]

    def place_x(which, carry):
        for second in range(counts[1]):
            start = (which * counts[1] + second) * counts[2]
            tiles = [slots[start + third] for third in range(counts[2])]
            for spot in range(per):
                value = jnp.zeros((8, LANES), F32)
                for third in range(counts[2]):
                    turn = (length[2] * (third - spot)) % LANES
                    moved = pltpu.roll(tiles[third], turn, 1) if turn else tiles[third]
                    value = jnp.where(lane // length[2] == third, moved, value)
                for group in range(8 // length[1]):
                    plane = which * length[0] + group * per + spot
                    whole[plane, second * length[1] : (second + 1) * length[1], :] = value[
                        group * length[1] : (group + 1) * length[1]
                    ]
        return carry

    lax.fori_loop(0, counts[0], place_x, 0)
    even_first = parity_of(first.rows, LANES)
    for number in range(first.count):
        one, two = whole[2 * number], whole[2 * number + 1]
        s.levels[0].f[number] = jnp.where(even_first, one, two)
        s.levels[0].g[number] = jnp.where(even_first, two, one)
    fill.wait()
    solve(plan, s, 0)
    solved = s.solved
    for number in range(3):
        solved[number] = jnp.zeros((first.rows, LANES), F32)
        solved[first.block[0] + 3 + number] = jnp.zeros((first.rows, LANES), F32)
    for plane in range(first.block[0]):
        solved[plane + 3] = first.planes(s.levels[0], even_first, plane)

    wait_all(plan, s, place, size_swap, SWAP + 1, other)
    wait_all(plan, s, place, size_swap, SWAP, other)
    shape = (LANES, LANES)
    index = iota(shape, 1)
    spot = local_of(index, plan.block1[2], 8, LANES)
    used = (index < plan.block1[2] + 8) | (index >= LANES - 8)
    lanes_to = weights(shape, (half_down(spot) + place[2] * length[2] == iota(shape, 0)) & used, 1.0)
    n = next_.count
    flat = jnp.concatenate([solved[place[0] * length[0] + number] for number in range(n)], axis=0)
    flat = dot(flat, lanes_to).reshape(n, first.rows, LANES)
    spread = s.spread
    spread[:, 0:16] = jnp.zeros((n, 16, LANES), F32)
    spread[:, 16 + 2 * first.rows :] = jnp.zeros((n, 16, LANES), F32)
    spread[0:n, pl.ds(16, first.rows, stride=2), :] = flat
    spread[0:n, pl.ds(17, first.rows, stride=2), :] = flat
    start = 16 + place[1] * rows1
    for number in range(n):
        tiles = [
            spread[number, pl.ds(pl.multiple_of(start + shift, 8), size), :]
            for shift, size in ((0, rows1), (rows1, 8), (-8, 8))
        ]
        s.next.B[number + 1] = swapped(plan, s, number) + jnp.concatenate(tiles, axis=0)
    for colour, skip in ((0, 0), (1, 1), (0, 1), (1, 2)):
        next_.half(s.next, colour, even_next, skip, n - skip)

    pick = iota((8, LANES), 0) < 4
    planes = []
    for number in range(count):
        value = next_.planes(s.next, even_next, number + 2 * next_.margins[0] - top.margins[0])
        edge = jnp.where(pick, value[rows1 : rows1 + 8], value[rows1 + 8 :])
        planes.append(jnp.concatenate([value[:rows1], edge], axis=0))
    shape = (LANES, top.lanes)
    cell, used = fine_cell(shape, 1)
    spreading = weights(shape, (cell == iota(shape, 0)) & used, 1.0)
    flat = dot(jnp.concatenate(planes, axis=0), spreading).reshape(count, plan.high, top.lanes)
    for tile in range(plan.tiles):
        piece = flat[:, :, tile * LANES : (tile + 1) * LANES]
        s.rows[tile][0:count, pl.ds(0, plan.high, stride=2), :] = piece
        s.rows[tile][0:count, pl.ds(1, plan.high, stride=2), :] = piece
    for number in range(count):
        tiles = []
        for tile in range(plan.tiles):
            rows = s.rows[tile]
            edge = jnp.where(pick, rows[number, block[1] : block[1] + 8], rows[number, block[1] + 8 : block[1] + 16])
            tiles.append(jnp.concatenate([rows[number, 0 : block[1]], edge], axis=0))
        s.top.B[number + 1] = s.top.B[number + 1] + jnp.concatenate(tiles, axis=1)
    top.half(s.top, 0, even_top, 0, count)
    top.half(s.top, 1, even_top, 1, count - 1)
    top.half(s.top, 0, even_top, 1, count - 1)
    red = s.top.R
    even_out = parity_of(block[1], block[2])
    for number, value in top.totals(red, even_top, 1, top.margins[0], count - top.margins[0]):
        black = ((s.top.g[number] + value) * inverse)[0 : block[1], 0 : block[2]]
        old = red[number + 1][0 : block[1], 0 : block[2]]
        plane = 2 * (number - top.margins[0])
        potential[plane] = jnp.where(even_out, old, black)
        potential[plane + 1] = jnp.where(even_out, black, old)
    wait_all(plan, s, place, size_part, PART, other)
    wait_all(plan, s, place, size_far, FAR, other)


def cycle_matrix(size, depth):
    def beside_sum(v):
        p = np.pad(v, ((0, 0), (1, 1), (1, 1), (1, 1)))
        total = p[:, 2:, 1:-1, 1:-1] + p[:, :-2, 1:-1, 1:-1] + p[:, 1:-1, 2:, 1:-1] + p[:, 1:-1, :-2, 1:-1]
        return total + along * (p[:, 1:-1, 1:-1, 2:] + p[:, 1:-1, 1:-1, :-2])

    def cycle(g, left):
        parity = np.indices(g.shape[1:]).sum(0) % 2

        def sweeps(v, number):
            for _ in range(number):
                for colour in (0, 1):
                    v = np.where(parity == colour, (g + beside_sum(v)) / centre, v)
            return v

        v = np.zeros_like(g)
        if left == 0:
            return sweeps(v, CSWEEPS)
        v = sweeps(v, 2)
        r = g - centre * v + beside_sum(v)
        x, y, z = (part // 2 for part in g.shape[1:])
        coarse = 4 * r.reshape(-1, x, 2, y, 2, z, 2).mean((2, 4, 6))
        e = cycle(coarse, left - 1)
        for dim in (1, 2, 3):
            e = np.repeat(e, 2, dim)
        return sweeps(v + e, 2)

    cells = size[0] * size[1] * size[2]
    found = cycle(np.eye(cells).reshape((cells,) + size), depth).reshape(cells, cells)
    parts = []
    for _ in range(3):
        parts.append(found.astype(np.float32).astype(jnp.bfloat16))
        found = found - parts[-1].astype(np.float64)
    return np.stack(parts)


def on_device(counts, density):
    plan = Plan(density.shape, counts)
    scratch, tree = jax.tree.flatten(plan.scratch())
    matrix = jnp.asarray(cycle_matrix(plan.dense, LEVELS - 1 - plan.dense_level))
    return pl.pallas_call(
        functools.partial(kernel, plan, tree),
        out_shape=jax.ShapeDtypeStruct(density.shape, F32),
        in_specs=[pl.BlockSpec(memory_space=pltpu.HBM)] * 2,
        out_specs=pl.BlockSpec(memory_space=pltpu.VMEM),
        scratch_shapes=scratch,
        compiler_params=pltpu.CompilerParams(
            collective_id=0, has_side_effects=True, vmem_limit_bytes=48 * 1024 * 1024
        ),
    )(
        pltpu.with_memory_space_constraint(density, pltpu.HBM),
        pltpu.with_memory_space_constraint(matrix, pltpu.HBM),
    )


def solution(mesh):
    counts = tuple(mesh.shape[axis] for axis in AXES)
    return jax.shard_map(
        functools.partial(on_device, counts),
        mesh=mesh,
        in_specs=(P("gx", "gy", "gz"),),
        out_specs=P("gx", "gy", "gz"),
        check_vma=False,
    )
```

time: 28.6 us -> 23.1 us (0.81)
  Pallas kernels: 25.4 us -> 22.3 us
  local copies, waits for them, and re-layouts: 3.06 us -> 0.71 us
    pallas_call x1, Pallas kernels: 25.4 us -> 22.3 us  [on_device(): pl.pallas_call(functools.partial(kernel, plan, tree), out_shape=jax.Shape...]
    unnamed x5 -> x1, local copies, waits for them, and re-layouts: 3.06 us -> 0.71 us
where the time goes in v2:
time: 23.1 us; the launch traced here: 23 us
  Pallas kernels  22.3 us (97%)
  local copies, waits for them, and re-layouts  0.71 us (3%)
    pallas_call x1, Pallas kernels, on_device(): pl.pallas_call(functools.partial(kernel, plan, tree), out_shape=jax.Shape...  22.3 us
    unnamed x1, local copies, waits for them, and re-layouts  0.71 us

profile of v2, /device:TPU:0, one launch (start us, length us, event | category | flops | bytes accessed | tf_op | source)
XLA Modules:
  0.0 23.0 jit_solution(17558296259833652202)
XLA Ops:
  0.0 22.3 %shard_map.28 = f32[32,16,128]{2,1,0:T(8,128)S(1)} custom-call(f32[32,16,128]{2,1,0:T(8,128)} %density.1, bf16[3,512,512]{2,1,0:T(8,128)(2,1)} %constant.2.clone.dense), custom_call_target="tpu_custom_call" | custom-call | tf_op jit(solution)/shard_map/pallas_call | solution.py:1017
  22.3 0.7 %copy.4 = f32[32,16,128]{2,1,0:T(8,128)} copy(f32[32,16,128]{2,1,0:T(8,128)S(1)} %shard_map.28) | data formatting | bytes 524288

commit v3 on v2

--- a/solution.py
+++ b/solution.py
@@ -62,42 +62,38 @@
     return jnp.where(value >= 0, lax.div(value, 2), -lax.div(1 - value, 2))
 
 
-def parity_of(rows, lanes):
-    return (iota((rows, lanes), 0) + iota((rows, lanes), 1)) % 2 == 0
-
-
-def beside(below, here, above, even, colour, edge):
-    rows, lanes = here.shape
-    down, up = pltpu.roll(here, 1, 0), pltpu.roll(here, rows - 1, 0)
-    left, right = pltpu.roll(here, 1, 1), pltpu.roll(here, lanes - 1, 1)
+def parity_of(rows, lanes, step=1):
+    return (iota((rows, lanes), 0) + iota((rows, lanes), 1) // step) % 2 == 0
+
+
+def beside(below, here, above, down, up, even, colour, edge, step):
+    lanes = here.shape[1]
+    left, right = pltpu.roll(here, step, 1), pltpu.roll(here, lanes - step, 1)
     if edge is not None:
-        if edge[0] == rows:
-            row = iota(here.shape, 0)
-            down = jnp.where(row == 0, 0.0, down)
-            up = jnp.where(row == rows - 1, 0.0, up)
-        if edge[1] == lanes:
+        if edge[1] * step == lanes:
             lane = iota(here.shape, 1)
-            left = jnp.where(lane == 0, 0.0, left)
-            right = jnp.where(lane == lanes - 1, 0.0, right)
+            left = jnp.where(lane < step, 0.0, left)
+            right = jnp.where(lane >= lanes - step, 0.0, right)
     other = jnp.where(even, below, above) if colour == 0 else jnp.where(even, above, below)
     return (here + other) + (down + up) + along * (left + right)
 
 
 class Grid:
-    def __init__(self, block, margins, edge=False):
-        self.block, self.margins = block, margins
+    def __init__(self, block, margins, edge=False, step=1):
+        self.block, self.margins, self.step = block, margins, step
         self.inner = block[0] // 2
         self.count = self.inner + 2 * margins[0]
         self.rows = up_to(block[1] + 2 * margins[1], 8)
         self.lanes = up_to(block[2] + 2 * margins[2], LANES)
         self.edge = (block[1], block[2]) if edge else None
+        self.tiles = self.lanes // LANES
 
     def scratch(self):
-        field = (self.count + 2, self.rows, self.lanes)
+        field = (self.count + 2, self.rows + 16, LANES)
         source = (self.count, self.rows, self.lanes)
         return dict(
-            R=pltpu.VMEM(field, F32),
-            B=pltpu.VMEM(field, F32),
+            R=[pltpu.VMEM(field, F32) for _ in range(self.tiles)],
+            B=[pltpu.VMEM(field, F32) for _ in range(self.tiles)],
             f=pltpu.VMEM(source, F32),
             g=pltpu.VMEM(source, F32),
             m=pltpu.VMEM((3, self.rows, self.lanes), F32),
@@ -109,10 +105,25 @@
         return 2 if number >= self.count - self.margins[0] else 1
 
     def guard(self, v):
-        empty = jnp.zeros((self.rows, self.lanes), F32)
-        for ref in (v.R, v.B):
+        empty = jnp.zeros((self.rows + 16, LANES), F32)
+        for ref in v.R + v.B:
             ref[0] = empty
             ref[self.count + 1] = empty
+            if self.edge:
+                ref[:, 0:8] = jnp.zeros((self.count + 2, 8, LANES), F32)
+                ref[:, self.rows + 8 :] = jnp.zeros((self.count + 2, 8, LANES), F32)
+
+    def get(self, field, number, shift=0):
+        parts = [ref[number, 8 + shift : 8 + shift + self.rows] for ref in field]
+        return parts[0] if len(parts) == 1 else jnp.concatenate(parts, axis=1)
+
+    def put(self, field, number, value):
+        for tile, ref in enumerate(field):
+            piece = value[:, tile * LANES : (tile + 1) * LANES]
+            ref[number, 8 : 8 + self.rows] = piece
+            if not self.edge:
+                ref[number, 0:8] = piece[self.rows - 8 :]
+                ref[number, 8 + self.rows :] = piece[0:8]
 
     def masks(self, v, place, counts):
         inside = None
@@ -120,6 +131,9 @@
         for dim in (1, 2):
             index = iota(shape, dim - 1)
             size = shape[dim - 1]
+            if dim == 2 and self.step > 1:
+                inside = inside & (index % self.step == 0) & (index < self.step * self.block[2])
+                continue
             margin, length = self.margins[dim], self.block[dim]
             used = (index < length + margin) | (index >= size - margin)
             spot = local_of(index, length, margin, size) + place[dim] * length
@@ -135,27 +149,28 @@
 
     def first(self, v, begin, end):
         for number in range(begin, end):
-            v.R[number + 1] = v.f[number] * v.m[self.zone(number)]
+            self.put(v.R, number + 1, v.f[number] * v.m[self.zone(number)])
 
     def totals(self, other, even, colour, begin, end):
-        before, here = other[begin], other[begin + 1]
+        before, here = self.get(other, begin), self.get(other, begin + 1)
         for number in range(begin, end):
-            after = other[number + 2]
-            yield number, beside(before, here, after, even, colour, self.edge)
+            after = self.get(other, number + 2)
+            down, up = self.get(other, number + 1, -1), self.get(other, number + 1, 1)
+            yield number, beside(before, here, after, down, up, even, colour, self.edge, self.step)
             before, here = here, after
 
     def half(self, v, colour, even, begin, end):
         target, other = (v.R, v.B) if colour == 0 else (v.B, v.R)
         source = v.f if colour == 0 else v.g
         for number, total in self.totals(other, even, colour, begin, end):
-            target[number + 1] = (source[number] + total) * v.m[self.zone(number)]
+            self.put(target, number + 1, (source[number] + total) * v.m[self.zone(number)])
 
     def residue(self, v, even, begin, end):
         for number, total in self.totals(v.B, even, 0, begin, end):
-            yield number, v.f[number] - centre * v.R[number + 1] + total
+            yield number, v.f[number] - centre * self.get(v.R, number + 1) + total
 
     def planes(self, v, even, plane):
-        red, black = v.R[plane // 2 + 1], v.B[plane // 2 + 1]
+        red, black = self.get(v.R, plane // 2 + 1), self.get(v.B, plane // 2 + 1)
         return jnp.where(even, red, black) if plane % 2 == 0 else jnp.where(even, black, red)
 
 
@@ -199,7 +214,7 @@
         size = tuple(block[which] * counts[which] // 4 for which in range(3))
         number = 2
         while size[0] * size[1] * size[2] > DENSE:
-            self.levels.append(Grid(size, (0, 0, 0), edge=True))
+            self.levels.append(Grid(size, (0, 0, 0), edge=True, step=1 << len(self.levels)))
             assert self.levels[-1].lanes == LANES
             size = tuple(part // 2 for part in size)
             number += 1
@@ -372,7 +387,7 @@
     rows = {0: (0, high, 0), 1: (high - 8, 8, high + 8), -1: (0, 8, high)}[dy]
     if dz == 0:
         planes = {0: (margin, inner, margin), 1: (inner, margin, 0), -1: (margin, margin, margin + inner)}[dx]
-        source = s.next.B.at[pl.ds(1 + planes[0], planes[1]), pl.ds(rows[0], rows[1]), :]
+        source = s.next.B[0].at[pl.ds(1 + planes[0], planes[1]), pl.ds(8 + rows[0], rows[1]), :]
         target = s.swap_land.at[pl.ds(planes[2], planes[1]), pl.ds(rows[2], rows[1]), :]
     else:
         side = (dz + 1) // 2
@@ -395,7 +410,7 @@
         begin = 0 if side == 0 else length - 8
         value = jnp.zeros(lane.shape, F32)
         for slot in range(plan.next.inner):
-            plane = s.next.B[1 + margin + slot, 0 : plan.block1[1], :]
+            plane = s.next.B[0][1 + margin + slot, 8 : 8 + plan.block1[1], :]
             value = jnp.where(lane // 8 == slot, pltpu.roll(plane, (8 * slot - begin) % LANES, 1), value)
         s.swap[side] = value
 
@@ -408,7 +423,7 @@
     slot = number - margin + (1 - which) * inner
     value = s.swap_land[number]
     if which == 1:
-        value = jnp.concatenate([s.next.B[number + 1, 0:rows, :], value[rows:]], axis=0)
+        value = jnp.concatenate([s.next.B[0][number + 1, 8 : 8 + rows, :], value[rows:]], axis=0)
     high = pltpu.roll(s.swap_side[0, which], (length - 8 * slot) % LANES, 1)
     low = pltpu.roll(s.swap_side[1, which], (LANES - 8 - 8 * slot) % LANES, 1)
     edge = jnp.where(lane < length + 8, high, jnp.where(lane >= LANES - 8, low, 0.0))
@@ -566,8 +581,8 @@
 
 def solve(plan, s, number):
     grid, v = plan.levels[number], s.levels[number]
-    even = parity_of(grid.rows, LANES)
-    count = grid.count
+    even = parity_of(grid.rows, LANES, grid.step)
+    count, step = grid.count, grid.step
     grid.first(v, 0, count)
     for colour in (1, 0, 1):
         grid.half(v, colour, even, 0, count)
@@ -579,30 +594,35 @@
         if grid.rows > grid.block[1]:
             value = jnp.where(iota(value.shape, 0) < grid.block[1], value, 0.0)
         pairs[spot, 0 : grid.rows] = value
-    flat = pair_sums(pairs, height, count).reshape(count * (height // 2), LANES)
+    sums = pair_sums(pairs, height, count)
     row, column = iota((LANES, LANES), 0), iota((LANES, LANES), 1)
     if number + 1 < len(plan.levels):
         below, under = plan.levels[number + 1], s.levels[number + 1]
-        down = weights((LANES, LANES), (row // 2 == column) & (row < grid.block[2]), 0.5)
-        coarse = dot(flat, down).reshape(count, height // 2, LANES)[:, : below.rows]
-        same = parity_of(below.rows, LANES)
+        same = parity_of(below.rows, LANES, below.step)
+        lane = iota((below.rows, LANES), 1)
+        coarse = []
+        for spot in range(count):
+            value = sums[spot][: below.rows]
+            value = 0.5 * (value + pltpu.roll(value, LANES - step, 1))
+            coarse.append(jnp.where((lane % below.step == 0) & (lane < step * grid.block[2]), value, 0.0))
         for spot in range(below.count):
             one, two = coarse[2 * spot], coarse[2 * spot + 1]
             under.f[spot] = jnp.where(same, one, two)
             under.g[spot] = jnp.where(same, two, one)
         solve(plan, s, number + 1)
-        planes = [below.planes(under, same, plane) for plane in range(count)]
-        spread = weights((LANES, LANES), column // 2 == row, 1.0)
-        flat = dot(jnp.concatenate(planes, axis=0), spread).reshape(count, below.rows, LANES)
-        pairs[0:count, pl.ds(0, below.rows, stride=2), :] = flat
-        pairs[0:count, pl.ds(1, below.rows, stride=2), :] = flat
         for spot in range(count):
-            v.B[spot + 1] = v.B[spot + 1] + pairs[spot, 0 : grid.rows]
+            plane = below.planes(under, same, spot)
+            plane = plane + pltpu.roll(plane, step, 1)
+            pairs[spot, pl.ds(0, below.rows, stride=2), :] = plane
+            pairs[spot, pl.ds(1, below.rows, stride=2), :] = plane
+        for spot in range(count):
+            grid.put(v.B, spot + 1, grid.get(v.B, spot + 1) + pairs[spot, 0 : grid.rows])
     else:
         nx, ny, nz = plan.dense
         size = nx * ny * nz
         tall = height // 2
-        down = weights((LANES, LANES), (row // 2 == column % nz) & (row < grid.block[2]), 0.5)
+        flat = sums.reshape(count * (height // 2), LANES)
+        down = weights((LANES, LANES), (row // (2 * step) == column % nz) & (row < step * grid.block[2]), 0.5)
         many = dot(flat, down).reshape(count, tall, LANES)
         wide = up_to(size, LANES) // LANES
         here, lane = iota((tall, LANES), 0), iota((tall, LANES), 1)
@@ -633,12 +653,43 @@
                 cell = (vector * LANES + lane) // nz
                 value = jnp.where(cell == spot * ny + here // 2, piece, value)
             planes.append(value)
-        spread = weights((LANES, LANES), (column // 2 == row % nz) & (column < grid.block[2]), 1.0)
+        spread = weights(
+            (LANES, LANES),
+            (column // (2 * step) == row % nz) & (column < step * grid.block[2]) & (column % step == 0),
+            1.0,
+        )
         flat = dot(jnp.concatenate(planes, axis=0), spread).reshape(count, grid.rows, LANES)
         for spot in range(count):
-            v.B[spot + 1] = v.B[spot + 1] + flat[spot]
+            grid.put(v.B, spot + 1, grid.get(v.B, spot + 1) + flat[spot])
     for colour in (0, 1, 0, 1):
         grid.half(v, colour, even, 0, count)
+
+
+def first_black(plan, s, even):
+    top, high, wide = plan.top, plan.block[1], plan.width
+    lane = iota((high, wide), 1)
+    none = jnp.zeros((high, LANES), F32)
+
+    def load(number, shift=0, begin=0, size=high):
+        parts = [ref[number, 8 + begin + shift : 8 + begin + shift + size] for ref in s.top.R[:-1]]
+        return parts[0] if len(parts) == 1 else jnp.concatenate(parts, axis=1)
+
+    for number in range(1, top.count - 1):
+        total = jnp.where(even, load(number + 2), load(number))
+        edge, side = jnp.zeros((8, wide), F32), none
+        if top.zone(number) == 1:
+            here = load(number + 1)
+            left, right = pltpu.roll(here, 1, 1), pltpu.roll(here, wide - 1, 1)
+            beside_z = jnp.where(lane == 0, 0.0, left) + jnp.where(lane == wide - 1, 0.0, right)
+            total = (here + total) + (load(number + 1, -1) + load(number + 1, 1)) + along * beside_z
+            total = total + s.top.g[number, 0:high, 0:wide]
+            edge = load(number + 1, -1, high, 8) + load(number + 1, 1, high, 8)
+            first, last = left[:, :LANES], right[:, wide - LANES :]
+            spot = lane[:, :LANES]
+            side = along * (jnp.where(spot == 0, first, 0.0) + jnp.where(spot == LANES - 1, last, 0.0))
+        side = jnp.concatenate([side, none[:8]], axis=0)
+        value = jnp.concatenate([jnp.concatenate([total, edge], axis=0), side], axis=1)
+        top.put(s.top.B, number + 1, value * s.top.m[top.zone(number)])
 
 
 def kernel(plan, tree, density, dense, potential, *refs):
@@ -680,7 +731,7 @@
     for off in offsets:
         pl.semaphore_signal(barrier, inc=1, device_id=peer(off, 0)[0], device_id_type=MESH)
 
-    for ref in (s.top.f, s.top.g, s.top.R, s.top.B):
+    for ref in [s.top.f, s.top.g] + s.top.R + s.top.B:
         ref[...] = jnp.zeros(ref.shape, F32)
     for v, grid in ((s.top, top), (s.wide, wide), (s.next, next_)):
         grid.guard(v)
@@ -703,10 +754,16 @@
         spot = number + top.margins[0]
         s.top.f[spot, 0 : block[1], 0 : plan.width] = red
         s.top.g[spot, 0 : block[1], 0 : plan.width] = jnp.where(even_own, two, one)
-        s.top.R[spot + 1, 0 : block[1], 0 : plan.width] = red * inverse
+        for tile in range(plan.width // LANES):
+            piece = red[:, tile * LANES : (tile + 1) * LANES] * inverse
+            s.top.R[tile][spot + 1, 8 : 8 + block[1]] = piece
+            s.top.R[tile][spot + 1, 8 + top.rows :] = piece[0:8]
     even_top = parity_of(top.rows, top.lanes)
     count = top.count
-    top.half(s.top, 1, even_top, 1, count - 1)
+    if top.lanes == plan.width + LANES:
+        first_black(plan, s, even_own)
+    else:
+        top.half(s.top, 1, even_top, 1, count - 1)
     top.half(s.top, 0, even_top, 1, count - 1)
     top.half(s.top, 1, even_top, 0, count)
     for number, value in top.residue(s.top, even_top, 0, count):
@@ -823,6 +880,17 @@
     pack_swap(plan, s)
     each(place, counts, swap)
 
+    def finish_sends():
+        for name in (ALL + 1, ALL):
+            pltpu.make_async_remote_copy(
+                src_ref=s.bytes.at[pl.ds(0, total - 1)],
+                dst_ref=s.bytes.at[pl.ds(0, total - 1)],
+                send_sem=sem(s, name),
+                recv_sem=sem(s, name),
+                device_id=other,
+                device_id_type=MESH,
+            ).wait_recv()
+
     wait_all(plan, s, place, size_far, FAR + 1, other)
     if not padded:
         loads[1].wait()
@@ -863,25 +931,15 @@
     for number in range(count):
         s.top.f[number] = narrow(s.wide.f[number + shift])
         s.top.g[number] = narrow(s.wide.g[number + shift])
-        s.top.B[number + 1] = narrow(s.wide.B[number + shift + 1])
-
-    def finish_sends():
-        for name in (ALL + 1, ALL):
-            pltpu.make_async_remote_copy(
-                src_ref=s.bytes.at[pl.ds(0, total - 1)],
-                dst_ref=s.bytes.at[pl.ds(0, total - 1)],
-                send_sem=sem(s, name),
-                recv_sem=sem(s, name),
-                device_id=other,
-                device_id_type=MESH,
-            ).wait_recv()
+        top.put(s.top.B, number + 1, narrow(wide.get(s.wide.B, number + shift + 1)))
 
     finish_sends()
+    fill.wait()
     lane = iota((8, LANES), 1)
     whole = s.whole
     first = plan.levels[0]
 
-    def place_x(which, carry):
+    def place_x(which):
         for second in range(counts[1]):
             start = (which * counts[1] + second) * counts[2]
             tiles = [slots[start + third] for third in range(counts[2])]
@@ -896,15 +954,14 @@
                     whole[plane, second * length[1] : (second + 1) * length[1], :] = value[
                         group * length[1] : (group + 1) * length[1]
                     ]
-        return carry
-
-    lax.fori_loop(0, counts[0], place_x, 0)
+
+    for which in range(counts[0]):
+        place_x(which)
     even_first = parity_of(first.rows, LANES)
     for number in range(first.count):
         one, two = whole[2 * number], whole[2 * number + 1]
         s.levels[0].f[number] = jnp.where(even_first, one, two)
         s.levels[0].g[number] = jnp.where(even_first, two, one)
-    fill.wait()
     solve(plan, s, 0)
     solved = s.solved
     for number in range(3):
@@ -934,7 +991,7 @@
             spread[number, pl.ds(pl.multiple_of(start + shift, 8), size), :]
             for shift, size in ((0, rows1), (rows1, 8), (-8, 8))
         ]
-        s.next.B[number + 1] = swapped(plan, s, number) + jnp.concatenate(tiles, axis=0)
+        next_.put(s.next.B, number + 1, swapped(plan, s, number) + jnp.concatenate(tiles, axis=0))
     for colour, skip in ((0, 0), (1, 1), (0, 1), (1, 2)):
         next_.half(s.next, colour, even_next, skip, n - skip)
 
@@ -958,7 +1015,7 @@
             rows = s.rows[tile]
             edge = jnp.where(pick, rows[number, block[1] : block[1] + 8], rows[number, block[1] + 8 : block[1] + 16])
             tiles.append(jnp.concatenate([rows[number, 0 : block[1]], edge], axis=0))
-        s.top.B[number + 1] = s.top.B[number + 1] + jnp.concatenate(tiles, axis=1)
+        top.put(s.top.B, number + 1, top.get(s.top.B, number + 1) + jnp.concatenate(tiles, axis=1))
     top.half(s.top, 0, even_top, 0, count)
     top.half(s.top, 1, even_top, 1, count - 1)
     top.half(s.top, 0, even_top, 1, count - 1)
@@ -966,7 +1023,7 @@
     even_out = parity_of(block[1], block[2])
     for number, value in top.totals(red, even_top, 1, top.margins[0], count - top.margins[0]):
         black = ((s.top.g[number] + value) * inverse)[0 : block[1], 0 : block[2]]
-        old = red[number + 1][0 : block[1], 0 : block[2]]
+        old = top.get(red, number + 1)[0 : block[1], 0 : block[2]]
         plane = 2 * (number - top.margins[0])
         potential[plane] = jnp.where(even_out, old, black)
         potential[plane + 1] = jnp.where(even_out, black, old)

time: 23.1 us -> 22.8 us (0.987)
  Pallas kernels: 22.3 us -> 22 us
    pallas_call x1, Pallas kernels: 22.3 us -> 22 us  [on_device(): pl.pallas_call(functools.partial(kernel, plan, tree), out_shape=jax.Shape...]
where the time goes in v3:
time: 22.8 us; the launch traced here: 22.7 us
  Pallas kernels  22 us (96%)
  local copies, waits for them, and re-layouts  0.71 us (3%)
    pallas_call x1, Pallas kernels, on_device(): pl.pallas_call(functools.partial(kernel, plan, tree), out_shape=jax.Shape...  22 us
    unnamed x1, local copies, waits for them, and re-layouts  0.71 us

profile of v3, /device:TPU:0, one launch (start us, length us, event | category | flops | bytes accessed | tf_op | source)
XLA Modules:
  0.0 22.7 jit_solution(10410772996433788803)
XLA Ops:
  0.0 22.0 %shard_map.28 = f32[32,16,128]{2,1,0:T(8,128)S(1)} custom-call(f32[32,16,128]{2,1,0:T(8,128)} %density.1, bf16[3,512,512]{2,1,0:T(8,128)(2,1)} %constant.2.clone.dense), custom_call_target="tpu_custom_call" | custom-call | tf_op jit(solution)/shard_map/pallas_call | solution.py:1074
  22.0 0.7 %copy.4 = f32[32,16,128]{2,1,0:T(8,128)} copy(f32[32,16,128]{2,1,0:T(8,128)S(1)} %shard_map.28) | data formatting | bytes 524288

commit v4 on v3

--- a/solution.py
+++ b/solution.py
@@ -26,7 +26,7 @@
 ]
 
 
-ALL, PART, FAR, SWAP, OWN, FIELD, MATRIX = 0, 2, 4, 6, 8, 9, 10
+ALL, PART, FAR, SWAP, OWN, FIELD, MATRIX, PAIR = 0, 2, 4, 6, 8, 9, 10, 11
 
 
 def up_to(value, unit):
@@ -141,6 +141,11 @@
             inside = used if inside is None else inside & used
         value = jnp.where(inside, inverse, 0.0).astype(F32)
         v.m[1] = value
+        if self.edge:
+            for zone, shift in ((0, -self.step), (2, self.step)):
+                spot = iota(shape, 1) + shift
+                kept = (spot >= 0) & (spot < self.step * self.block[2]) & (iota(shape, 1) % self.step == 0)
+                v.m[zone] = jnp.where(kept & (iota(shape, 0) < self.block[1]), inverse, 0.0).astype(F32)
         if self.margins[0]:
             low = jnp.where(place[0] > 0, 1.0, 0.0).astype(F32)
             high = jnp.where(place[0] < counts[0] - 1, 1.0, 0.0).astype(F32)
@@ -164,6 +169,30 @@
         source = v.f if colour == 0 else v.g
         for number, total in self.totals(other, even, colour, begin, end):
             self.put(target, number + 1, (source[number] + total) * v.m[self.zone(number)])
+
+    def pair(self, v, even):
+        step, lanes = self.step, self.lanes
+        lane = iota((self.rows, lanes), 1)
+        sides = []
+        for number in range(self.count):
+            here = self.get(v.B, number + 1)
+            other = jnp.where(even, self.get(v.B, number), self.get(v.B, number + 2))
+            rows = self.get(v.B, number + 1, -1) + self.get(v.B, number + 1, 1)
+            total = v.f[number] + ((here + other) + rows)
+            left = jnp.where(lane < step, 0.0, pltpu.roll(here, step, 1))
+            right = jnp.where(lane >= lanes - step, 0.0, pltpu.roll(here, lanes - step, 1))
+            second = jnp.where(lane < 2 * step, 0.0, pltpu.roll(here, 2 * step, 1))
+            third = jnp.where(lane >= lanes - 2 * step, 0.0, pltpu.roll(here, lanes - 2 * step, 1))
+            self.put(v.R, number + 1, (total + along * (left + right)) * v.m[1])
+            before = (pltpu.roll(total, step, 1) + along * (second + here)) * v.m[0]
+            after = (pltpu.roll(total, lanes - step, 1) + along * (here + third)) * v.m[2]
+            sides.append(before + after)
+        for number in range(self.count):
+            here = self.get(v.R, number + 1)
+            other = jnp.where(even, self.get(v.R, number + 2), self.get(v.R, number))
+            rows = self.get(v.R, number + 1, -1) + self.get(v.R, number + 1, 1)
+            total = v.g[number] + ((here + other) + rows)
+            self.put(v.B, number + 1, (total + along * sides[number]) * v.m[1])
 
     def residue(self, v, even, begin, end):
         for number, total in self.totals(v.B, even, 0, begin, end):
@@ -275,7 +304,7 @@
         s.matrix = pltpu.VMEM((3, size, size), BF16)
         most = max(sum(size(self, steps) for steps in DIRECTIONS) for size in (size_part, size_far, size_swap))
         s.bytes = pltpu.VMEM((max(most, self.total), 8, LANES), F32)
-        s.sem = pltpu.SemaphoreType.DMA((MATRIX + 1,))
+        s.sem = pltpu.SemaphoreType.DMA((PAIR + 2,))
         return vars(s)
 
 
@@ -584,8 +613,17 @@
     even = parity_of(grid.rows, LANES, grid.step)
     count, step = grid.count, grid.step
     grid.first(v, 0, count)
-    for colour in (1, 0, 1):
-        grid.half(v, colour, even, 0, count)
+    small = count * grid.rows <= 64
+
+    def sweep():
+        if small:
+            grid.pair(v, even)
+            return
+        grid.half(v, 0, even, 0, count)
+        grid.half(v, 1, even, 0, count)
+
+    grid.half(v, 1, even, 0, count)
+    sweep()
     pairs = s.pairs
     height = max(grid.rows, 16)
     if grid.rows < height:
@@ -661,8 +699,8 @@
         flat = dot(jnp.concatenate(planes, axis=0), spread).reshape(count, grid.rows, LANES)
         for spot in range(count):
             grid.put(v.B, spot + 1, grid.get(v.B, spot + 1) + flat[spot])
-    for colour in (0, 1, 0, 1):
-        grid.half(v, colour, even, 0, count)
+    sweep()
+    sweep()
 
 
 def first_black(plan, s, even):
@@ -698,7 +736,14 @@
     counts, block, total = plan.counts, plan.block, plan.total
     top, wide, next_ = plan.top, plan.wide, plan.next
     place = tuple(lax.axis_index(axis) for axis in AXES)
-    me = (place[0] * counts[1] + place[1]) * counts[2] + place[2]
+    paired = counts[2] % 2 == 0
+    kinds = 2 if paired else 1
+
+    def slot_of(x, y, z):
+        kind, rest = (lax.rem(z, 2), lax.div(z, 2)) if paired and not isinstance(z, int) else (z % kinds, z // kinds)
+        return kind * (total // kinds) + (x * counts[1] + y) * (counts[2] // kinds) + rest
+
+    me = slot_of(*place)
     padded = block[2] != plan.width
 
     loads = [pltpu.make_async_copy(density, s.raw if padded else s.own, sem(s, OWN))]
@@ -724,7 +769,7 @@
 
     def peer(off, way):
         target = tuple(axes[axis][off[axis]][way] for axis in range(3))
-        return target, (target[0] * counts[1] + target[1]) * counts[2] + target[2]
+        return target, slot_of(*target)
 
     other = peer(offsets[0], 0)[0]
     barrier = pltpu.get_barrier_semaphore()
@@ -871,9 +916,23 @@
             device_id_type=MESH,
         )
 
+    chosen = [number for number, off in enumerate(offsets) if off[2] % kinds == 0]
+
     def start_sends():
-        for number in range(total - 1):
+        for number in chosen:
             send(number, me).start()
+
+    def forward():
+        half = total // 2
+        kind = lax.rem(place[2], 2) * half
+        return pltpu.make_async_remote_copy(
+            src_ref=slots.at[pl.ds(kind, half)],
+            dst_ref=slots.at[pl.ds(kind, half)],
+            send_sem=sem(s, PAIR),
+            recv_sem=sem(s, PAIR + 1),
+            device_id=peer((0, 0, 1), 0)[0],
+            device_id_type=MESH,
+        )
 
     start_sends()
     swap = functools.partial(send_swap, plan, s, place)
@@ -883,8 +942,8 @@
     def finish_sends():
         for name in (ALL + 1, ALL):
             pltpu.make_async_remote_copy(
-                src_ref=s.bytes.at[pl.ds(0, total - 1)],
-                dst_ref=s.bytes.at[pl.ds(0, total - 1)],
+                src_ref=s.bytes.at[pl.ds(0, len(chosen))],
+                dst_ref=s.bytes.at[pl.ds(0, len(chosen))],
                 send_sem=sem(s, name),
                 recv_sem=sem(s, name),
                 device_id=other,
@@ -934,6 +993,9 @@
         top.put(s.top.B, number + 1, narrow(wide.get(s.wide.B, number + shift + 1)))
 
     finish_sends()
+    if paired:
+        forward().start()
+        forward().wait()
     fill.wait()
     lane = iota((8, LANES), 1)
     whole = s.whole
@@ -941,8 +1003,7 @@
 
     def place_x(which):
         for second in range(counts[1]):
-            start = (which * counts[1] + second) * counts[2]
-            tiles = [slots[start + third] for third in range(counts[2])]
+            tiles = [slots[slot_of(which, second, third)] for third in range(counts[2])]
             for spot in range(per):
                 value = jnp.zeros((8, LANES), F32)
                 for third in range(counts[2]):

time: 22.8 us -> 22.6 us (level)
  no operation moved by 1% of the time
where the time goes in v4:
time: 22.6 us; the launch traced here: 22.5 us
  Pallas kernels  21.8 us (96%)
  local copies, waits for them, and re-layouts  0.71 us (3%)
    pallas_call x1, Pallas kernels, on_device(): pl.pallas_call(functools.partial(kernel, plan, tree), out_shape=jax.Shape...  21.8 us
    unnamed x1, local copies, waits for them, and re-layouts  0.71 us

profile of v4, /device:TPU:0, one launch (start us, length us, event | category | flops | bytes accessed | tf_op | source)
XLA Modules:
  0.0 22.5 jit_solution(13176230404196202581)
XLA Ops:
  0.0 21.8 %shard_map.28 = f32[32,16,128]{2,1,0:T(8,128)S(1)} custom-call(f32[32,16,128]{2,1,0:T(8,128)} %density.1, bf16[3,512,512]{2,1,0:T(8,128)(2,1)} %constant.2.clone.dense), custom_call_target="tpu_custom_call" | custom-call | tf_op jit(solution)/shard_map/pallas_call | solution.py:1135
  21.8 0.7 %copy.4 = f32[32,16,128]{2,1,0:T(8,128)} copy(f32[32,16,128]{2,1,0:T(8,128)S(1)} %shard_map.28) | data formatting | bytes 524288

commit v5 on v4

--- a/solution.py
+++ b/solution.py
@@ -773,8 +773,27 @@
 
     other = peer(offsets[0], 0)[0]
     barrier = pltpu.get_barrier_semaphore()
+    close = max(counts) <= 4
+    waited = total - 1
+    if close:
+        waited = 1
+        for axis in range(3):
+            waited = waited * (1 + jnp.minimum(place[axis], 2) + jnp.minimum(counts[axis] - 1 - place[axis], 2))
+        waited = waited - 1
     for off in offsets:
-        pl.semaphore_signal(barrier, inc=1, device_id=peer(off, 0)[0], device_id_type=MESH)
+        target = peer(off, 0)[0]
+        apart = [target[axis] - place[axis] for axis in range(3) if off[axis] and counts[axis] > 3]
+        near = None
+        for step in apart if close else []:
+            here = (step <= 2) & (step >= -2)
+            near = here if near is None else near & here
+        if near is None:
+            pl.semaphore_signal(barrier, inc=1, device_id=target, device_id_type=MESH)
+            continue
+
+        @pl.when(near)
+        def _():
+            pl.semaphore_signal(barrier, inc=1, device_id=target, device_id_type=MESH)
 
     for ref in [s.top.f, s.top.g] + s.top.R + s.top.B:
         ref[...] = jnp.zeros(ref.shape, F32)
@@ -836,7 +855,7 @@
     s.part[...] = dot(flat, down).reshape(count, plan.high, LANES)
     pack_part(plan, s)
 
-    pl.semaphore_wait(barrier, total - 1)
+    pl.semaphore_wait(barrier, waited)
     part = functools.partial(send_part, plan, s, place)
     far = functools.partial(send_far, plan, s, place)
     each(place, counts, part)

time: 22.6 us -> 22.6 us (level)
  no operation moved by 1% of the time
where the time goes in v5:
time: 22.6 us; the launch traced here: 22.5 us
  Pallas kernels  21.8 us (96%)
  local copies, waits for them, and re-layouts  0.71 us (3%)
    pallas_call x1, Pallas kernels, on_device(): pl.pallas_call(functools.partial(kernel, plan, tree), out_shape=jax.Shape...  21.8 us
    unnamed x1, local copies, waits for them, and re-layouts  0.71 us

profile of v5, /device:TPU:0, one launch (start us, length us, event | category | flops | bytes accessed | tf_op | source)
XLA Modules:
  0.0 22.5 jit_solution(1523037097250645019)
XLA Ops:
  0.0 21.8 %shard_map.28 = f32[32,16,128]{2,1,0:T(8,128)S(1)} custom-call(f32[32,16,128]{2,1,0:T(8,128)} %density.1, bf16[3,512,512]{2,1,0:T(8,128)(2,1)} %constant.2.clone.dense), custom_call_target="tpu_custom_call" | custom-call | tf_op jit(solution)/shard_map/pallas_call | solution.py:1154
  21.8 0.7 %copy.4 = f32[32,16,128]{2,1,0:T(8,128)} copy(f32[32,16,128]{2,1,0:T(8,128)S(1)} %shard_map.28) | data formatting | bytes 524288

commit v6 on v5

--- a/solution.py
+++ b/solution.py
@@ -855,11 +855,6 @@
     s.part[...] = dot(flat, down).reshape(count, plan.high, LANES)
     pack_part(plan, s)
 
-    pl.semaphore_wait(barrier, waited)
-    part = functools.partial(send_part, plan, s, place)
-    far = functools.partial(send_far, plan, s, place)
-    each(place, counts, part)
-
     lane = iota((block[1], LANES), 1)
     for side in range(2):
         begin = 0 if side == 0 else block[2] - 8
@@ -871,6 +866,11 @@
                 moved = pltpu.roll(plane, (8 * slot - begin) % LANES, 1)
                 value = jnp.where(lane // 8 == slot, moved, value)
             s.far[side, pack] = value
+    pl.semaphore_wait(barrier, waited)
+    part = functools.partial(send_part, plan, s, place)
+    far = functools.partial(send_far, plan, s, place)
+    each(place, counts, part)
+
     each(place, counts, far)
     field, far_land = s.field, s.far_land
     if padded:

time: 22.6 us -> 22.7 us (level)
  no operation moved by 1% of the time
where the time goes in v6:
time: 22.7 us; the launch traced here: 22.5 us
  Pallas kernels  21.8 us (96%)
  local copies, waits for them, and re-layouts  0.71 us (3%)
    pallas_call x1, Pallas kernels, on_device(): pl.pallas_call(functools.partial(kernel, plan, tree), out_shape=jax.Shape...  21.8 us
    unnamed x1, local copies, waits for them, and re-layouts  0.71 us

profile of v6, /device:TPU:0, one launch (start us, length us, event | category | flops | bytes accessed | tf_op | source)
XLA Modules:
  0.0 22.5 jit_solution(11536797396609783933)
XLA Ops:
  0.0 21.8 %shard_map.28 = f32[32,16,128]{2,1,0:T(8,128)S(1)} custom-call(f32[32,16,128]{2,1,0:T(8,128)} %density.1, bf16[3,512,512]{2,1,0:T(8,128)(2,1)} %constant.2.clone.dense), custom_call_target="tpu_custom_call" | custom-call | tf_op jit(solution)/shard_map/pallas_call | solution.py:1154
  21.8 0.7 %copy.4 = f32[32,16,128]{2,1,0:T(8,128)} copy(f32[32,16,128]{2,1,0:T(8,128)S(1)} %shard_map.28) | data formatting | bytes 524288
